TPU v7x, 8 devices: a whole 2x2x1 slice. The times are simulated.
8 devices in a mesh: dp: 2 (over z, y), ep: 4 (over x, core).
Axes of the slice: x: 2, y: 2, z: 1, core: 2. Of those that a mesh axis runs over, the one named last changes fastest.
Arguments:
- tokens: bfloat16 [8, 512, 2048], P(('dp', 'ep')), parts along dimension 0
- w_query: bfloat16 [2048, 16, 128], P('ep')
- w_key: bfloat16 [2048, 16, 128], P('ep')
- w_value: bfloat16 [2048, 16, 128], P('ep')
- w_out: bfloat16 [2048, 2048], P('ep')
- w_router: float32 [2048, 64], replicated
- w_one: bfloat16 [64, 2048, 1024], P('ep')
- w_three: bfloat16 [64, 2048, 1024], P('ep')
- w_two: bfloat16 [64, 1024, 2048], P('ep')
- expert_ids: int32 [8, 512, 8], P(('dp', 'ep')), parts along dimension 0
Outputs:
- output: bfloat16 [8, 512, 2048], P(('dp', 'ep')), parts along dimension 0
There are 2 independent parts. A program takes and returns all parts, laid end to end along the dimension named above; an argument that names none is the same for every part.
All inputs are finite; a program needn't handle non-finite values.
Results may differ from a plain program's by a relative error of at most 0.00977733.
Values are sent between devices in bfloat16 or wider.
A program may use at most 1 GiB of HBM per device.

v0:
```python
import jax
import jax.numpy as jnp
from jax import lax
from jax.sharding import PartitionSpec as P

EPS = 1e-6


def rms_norm(vals):
    wide = vals.astype(jnp.float32)
    return wide * lax.rsqrt(jnp.mean(wide * wide, axis=-1, keepdims=True) + EPS)


def attention_layer(tokens, w_query, w_key, w_value, w_out):
    seq_count = tokens.shape[0]
    seq_len = tokens.shape[1]
    head_dim = w_query.shape[2]
    normed = rms_norm(tokens).astype(jnp.bfloat16)
    query = jnp.einsum('bsd,dhk->bshk', normed, w_query, preferred_element_type=jnp.float32).astype(jnp.bfloat16)
    keys = jnp.einsum('bsd,dhk->bshk', normed, w_key, preferred_element_type=jnp.float32).astype(jnp.bfloat16)
    values = jnp.einsum('bsd,dhk->bshk', normed, w_value, preferred_element_type=jnp.float32).astype(jnp.bfloat16)
    scores = jnp.einsum('bqhk,bshk->bhqs', query, keys, preferred_element_type=jnp.float32) * head_dim ** -0.5
    causal = lax.broadcasted_iota(jnp.int32, (seq_len, seq_len), 0) >= lax.broadcasted_iota(jnp.int32, (seq_len, seq_len), 1)
    attn_weights = jax.nn.softmax(jnp.where(causal, scores, -jnp.inf), axis=-1).astype(jnp.bfloat16)
    context = jnp.einsum('bhqs,bshk->bqhk', attn_weights, values, preferred_element_type=jnp.float32).astype(jnp.bfloat16)
    attn_out = jnp.einsum('crd,de->cre', context.reshape(seq_count, seq_len, -1), w_out, preferred_element_type=jnp.float32)
    return (tokens.astype(jnp.float32) + attn_out).astype(jnp.bfloat16)


def router_gates(hidden, w_router, expert_ids):
    normed = rms_norm(hidden)
    logits = jnp.einsum('bsd,de->bse', normed, w_router, precision=lax.Precision.HIGHEST, preferred_element_type=jnp.float32)
    chosen = jnp.take_along_axis(logits, expert_ids, axis=-1)
    return normed.astype(jnp.bfloat16), jax.nn.softmax(chosen, axis=-1)


def dispatch_tables(ids_flat, experts, cap_rows):
    member = jnp.sum((ids_flat[:, :, None] == jnp.arange(experts, dtype=jnp.int32)).astype(jnp.int32), axis=1)
    before = jnp.cumsum(member, axis=0) - member
    slot = jnp.take_along_axis(before, ids_flat, axis=1)
    onehot = (member[:, :, None] > 0) & (before[:, :, None] == jnp.arange(cap_rows, dtype=jnp.int32))
    return onehot.astype(jnp.bfloat16), ids_flat * cap_rows + slot


def expert_ffn(rows, w_one, w_three, w_two):
    first = jnp.einsum('end,edf->enf', rows, w_one, preferred_element_type=jnp.float32)
    third = jnp.einsum('end,edf->enf', rows, w_three, preferred_element_type=jnp.float32)
    activated = (jax.nn.silu(first) * third).astype(jnp.bfloat16)
    return jnp.einsum('enf,efd->end', activated, w_two, preferred_element_type=jnp.float32).astype(jnp.bfloat16)


def combine_rows(hidden_flat, back_rows, flat_slot, gates_flat):
    table = back_rows.reshape(-1, back_rows.shape[-1])
    picked = jnp.take(table, flat_slot, axis=0)
    mixed = jnp.sum(gates_flat[:, :, None] * picked.astype(jnp.float32), axis=1)
    return (hidden_flat.astype(jnp.float32) + mixed).astype(jnp.bfloat16)


def solution(mesh):
    tok_spec = P(('dp', 'ep'))
    row_spec = P('ep')

    def local_layer(tokens, w_query, w_key, w_value, w_out, w_router, w_one, w_three, w_two, expert_ids):
        full_query = lax.all_gather(w_query, 'ep', axis=0, tiled=True)
        full_key = lax.all_gather(w_key, 'ep', axis=0, tiled=True)
        full_value = lax.all_gather(w_value, 'ep', axis=0, tiled=True)
        full_out = lax.all_gather(w_out, 'ep', axis=0, tiled=True)
        hidden = attention_layer(tokens, full_query, full_key, full_value, full_out)
        normed, gates = router_gates(hidden, w_router, expert_ids)
        seq_count, seq_len, model_dim = tokens.shape
        choices = expert_ids.shape[2]
        experts = w_router.shape[1]
        tok_count = seq_count * seq_len
        cap_rows = 2 * tok_count * choices // experts
        onehot, flat_slot = dispatch_tables(expert_ids.reshape(tok_count, choices), experts, cap_rows)
        send_rows = jnp.einsum('tec,td->ecd', onehot, normed.reshape(tok_count, model_dim), preferred_element_type=jnp.float32).astype(jnp.bfloat16)
        recv_rows = lax.all_to_all(send_rows, 'ep', 0, 1, tiled=True)
        done_rows = expert_ffn(recv_rows, w_one, w_three, w_two)
        back_rows = lax.all_to_all(done_rows, 'ep', 1, 0, tiled=True)
        layer_out = combine_rows(hidden.reshape(tok_count, model_dim), back_rows, flat_slot, gates.reshape(tok_count, choices))
        return layer_out.reshape(seq_count, seq_len, model_dim)

    return jax.shard_map(local_layer, mesh=mesh, in_specs=(tok_spec, row_spec, row_spec, row_spec, row_spec, P(), row_spec, row_spec, row_spec, tok_spec), out_specs=tok_spec, check_vma=False)
```

profile of v0, /device:TPU:0, one launch (start us, length us, event | category | flops | bytes accessed | tf_op | source)
XLA Modules:
  0.0 1371.3 jit_solution(8719876065099649381)
XLA Ops:
  6.5 0.7 all-gather.7.cloned.1.call-update
  7.3 0.7 all-gather.9.cloned.1.call-update
  8.1 0.7 all-gather.5.cloned.1.call-update
  8.8 0.5 all-gather.11.cloned.1.call-update
  9.3 0.1 convert_reduce_fusion
  9.5 1.2 reduce-window.6
  10.7 0.2 slice_reduce_fusion
  11.1 0.5 fusion.20
  11.6 0.1 fusion.47
  11.7 55.8 %all-gather.7.cloned.1.call-done = bf16[2048,16,128]{2,1,0:T(8,128)(2,1)} async-done(((bf16[512,16,128]{2,1,0:T(8,128)(2,1)}), bf16[2048,16,128]{2,1,0:T(8,128)(2,1)}) %all-gather.7.cloned.1.call-update) | async-done | bytes 8388624 | tf_op jit(solution)/shard_map/all_gather | solution.py:64
  67.5 9.3 fusion.6
  76.7 48.0 %all-gather.9.cloned.1.call-done = bf16[2048,16,128]{2,1,0:T(8,128)(2,1)} async-done(((bf16[512,16,128]{2,1,0:T(8,128)(2,1)}), bf16[2048,16,128]{2,1,0:T(8,128)(2,1)}) %all-gather.9.cloned.1.call-update) | async-done | bytes 8388624 | tf_op jit(solution)/shard_map/all_gather | solution.py:65
  124.7 12.7 fusion.30
  137.4 17.2 %fusion.59 = (f32[16,512]{1,0:T(8,128)S(1)}, f32[16,512,512]{1,2,0:T(8,128)}) fusion(f32[16,512,512]{1,2,0:T(8,128)} %fusion.30, pred[512,512]{0,1:T(8,128)(4,1)S(1)} %iota_compare_fusion.2), kind=kOutput, calls=%fused_computation.81 | output fusion | flops 25166336 | bytes 33849344 | tf_op jit(solution)/shard_map/sub | solution.py:24
  154.7 27.3 %all-gather.5.cloned.1.call-done = bf16[2048,16,128]{2,1,0:T(8,128)(2,1)} async-done(((bf16[512,16,128]{2,1,0:T(8,128)(2,1)}), bf16[2048,16,128]{2,1,0:T(8,128)(2,1)}) %all-gather.5.cloned.1.call-update) | async-done | bytes 8388624 | tf_op jit(solution)/shard_map/all_gather | solution.py:66
  182.0 12.6 fusion.42
  194.6 44.6 %all-gather.11.cloned.1.call-done = bf16[2048,2048]{1,0:T(8,128)(2,1)} async-done(((bf16[512,2048]{1,0:T(8,128)(2,1)}), bf16[2048,2048]{1,0:T(8,128)(2,1)}) %all-gather.11.cloned.1.call-update) | async-done | bytes 8388624 | tf_op jit(solution)/shard_map/all_gather | solution.py:67
  239.2 9.0 fusion.23
  248.2 22.0 %convolution_convert_fusion = bf16[64,128,2048]{2,1,0:T(8,128)(2,1)} fusion(s32[512,64]{0,1:T(8,128)S(1)} %fusion.47, pred[512,64]{0,1:T(8,128)(4,1)S(1)} %broadcast_compare_fusion, bf16[1,512,2048]{2,1,0:T(8,128)(2,1)S(1)} %get-tuple-element.10, f32[512]{0:T(512)S(1)} %add_rsqrt_fusion), kind=kOutput, calls=%fused_computation.6 | convolution fusion | flops 17208180736 | bytes 35817472 | tf_op jit(solution)/shard_map/tec,td->ecd/dot_general | solution.py:76
  270.2 380.8 %all_to_all.33 = bf16[64,128,2048]{2,1,0:T(8,128)(2,1)} all-to-all(bf16[64,128,2048]{2,1,0:T(8,128)(2,1)} %convolution_convert_fusion), channel_id=1, replica_groups=mesh['dp'=2,'ep'=4] {'ep'}, dimensions={0} | all-to-all | bytes 67108864 | tf_op jit(solution)/shard_map/all_to_all | solution.py:77
  651.0 22.9 %copy.77 = bf16[16,4,128,2048]{3,2,1,0:T(8,128)(2,1)} copy(bf16[16,4,128,2048]{3,2,0,1:T(8,128)(2,1)} %bitcast.91) | data formatting | bytes 67108864 | tf_op jit(solution)/shard_map/all_to_all | solution.py:77
  673.9 56.7 %fusion.60 = f32[16,512,1024]{2,1,0:T(8,128)} fusion(bf16[16,512,2048]{2,1,0:T(8,128)(2,1)} %bitcast.92, bf16[16,2048,1024]{2,1,0:T(8,128)(2,1)} %param.16), kind=kOutput, calls=%fused_computation.82 | convolution fusion | flops 34359738368 | bytes 134217728 | tf_op jit(solution)/shard_map/end,edf->enf/dot_general | solution.py:46
  730.6 85.4 %convolution_convert_fusion.1 = bf16[16,512,2048]{2,1,0:T(8,128)(2,1)} fusion(bf16[16,1024,2048]{2,1,0:T(8,128)(2,1)} %param.18, f32[16,512,1024]{2,1,0:T(8,128)} %fusion.60, bf16[16,512,2048]{2,1,0:T(8,128)(2,1)} %bitcast.93, bf16[16,2048,1024]{2,1,0:T(8,128)(2,1)} %param.17), kind=kOutput, calls=%fused_computation.7 | convolution fusion | flops 68786585600 | bytes 234881024 | tf_op jit(solution)/shard_map/enf,efd->end/dot_general | solution.py:49
  816.0 30.0 %copy.78 = bf16[16,512,2048]{2,0,1:T(8,128)(2,1)} copy(bf16[16,512,2048]{2,1,0:T(8,128)(2,1)} %convolution_convert_fusion.1) | data formatting | bytes 67108864 | tf_op jit(solution)/shard_map/convert_element_type | solution.py:49
  846.1 10.1 all-to-all-start.1
  856.2 0.1 copy.74
  856.4 0.2 reshape.270
  856.5 0.6 copy-done.2
  857.1 33.0 %gather_fusion.2 = s32[4096]{0:T(1024)S(1)} fusion(s32[512,64]{0,1:T(8,128)S(1)} %copy-done.2, s32[4096]{0:T(1024)S(1)} %reshape.270), kind=kCustom, calls=%fused_computation.2 | custom fusion | bytes 65536 | tf_op jit(solution)/shard_map/jit(take_along_axis)/gather | solution.py:40
  890.2 0.2 gather.16
  890.3 0.2 reshape.273
  890.5 0.1 copy.80
  890.6 0.1 copy.81
  890.7 0.2 reshape.256
  890.9 0.1 copy.69
  891.0 0.2 reshape.264
  891.2 0.1 copy.75
  891.3 0.2 copy.76
  891.5 4.4 fusion.18
  896.0 33.0 %gather_fusion.1 = f32[4096]{0:T(1024)S(1)} fusion(f32[512,64]{0,1:T(8,128)S(1)} %fusion.18, s32[4096]{0:T(1024)S(1)} %reshape.264), kind=kCustom, calls=%fused_computation.1 | custom fusion | bytes 65536 | tf_op jit(solution)/shard_map/jit(take_along_axis)/gather | solution.py:33
  929.0 0.2 reshape.263
  929.2 0.1 copy.70
  929.3 0.1 copy.71
  929.5 289.2 %all-to-all-done.1 = bf16[16,512,2048]{2,0,1:T(8,128)(2,1)} async-done(((bf16[16,512,2048]{2,0,1:T(8,128)(2,1)}), bf16[16,512,2048]{2,0,1:T(8,128)(2,1)}, u32[]{:S(2)}, u32[]{:S(2)}) %all-to-all-start.1) | async-done | bytes 33554464 | tf_op jit(solution)/shard_map/all_to_all | solution.py:79
  1218.7 30.1 %copy.79 = bf16[16,4,128,2048]{3,2,0,1:T(8,128)(2,1)} copy(bf16[16,4,128,2048]{3,0,2,1:T(8,128)(2,1)} %bitcast.18) | data formatting | bytes 67108864 | tf_op jit(solution)/shard_map/all_to_all | solution.py:79
  1248.8 95.9 %gather_fusion = bf16[4096,2048]{1,0:T(8,128)(2,1)} fusion(bf16[8192,2048]{1,0:T(8,128)(2,1)} %bitcast.90, s32[4096]{0:T(1024)S(1)} %broadcast_clamp_fusion), kind=kCustom, calls=%fused_computation | custom fusion | bytes 33570816 | tf_op jit(solution)/shard_map/jit(_take)/gather | solution.py:54
  1344.7 17.6 %multiply_reduce_fusion = f32[512,2048]{1,0:T(8,128)S(1)} fusion(bf16[4096,2048]{1,0:T(8,128)(2,1)} %gather_fusion, f32[512,8]{1,0:T(8,128)S(1)} %copy.71, pred[512,8]{1,0:T(8,128)(4,1)S(1)} %copy.76), kind=kLoop, calls=%fused_computation.4 | loop fusion | flops 32505856 | bytes 20992000 | tf_op jit(solution)/shard_map/reduce_sum | solution.py:55
  1362.3 2.1 fusion.24
  (37 shorter events, 0.5 us)
Async XLA Ops:
  6.5 884.9 %copy-start = (f32[2048,64]{0,1:T(8,128)S(1)}, f32[2048,64]{0,1:T(8,128)}, u32[]{:S(2)}) copy-start(f32[2048,64]{0,1:T(8,128)} %param.15) | copy-start | bytes 1572868
  6.5 2.8 copy-start.6
  6.5 60.9 %all-gather.7.cloned.1.call-start = ((), (), s32[]{:S(2)}) async-start(), calls=%async_computation.3 | async-start | bytes 10485760 | tf_op jit(solution)/shard_map/all_gather | solution.py:64
  7.3 3.8 copy-start.5
  7.3 117.5 %all-gather.9.cloned.1.call-start = ((), (), s32[]{:S(2)}) async-start(), calls=%async_computation.4 | async-start | bytes 10485760 | tf_op jit(solution)/shard_map/all_gather | solution.py:65
  8.0 174.0 %all-gather.5.cloned.1.call-start = ((), (), s32[]{:S(2)}) async-start(), calls=%async_computation.2 | async-start | bytes 10485760 | tf_op jit(solution)/shard_map/all_gather | solution.py:66
  8.8 230.4 %all-gather.11.cloned.1.call-start = ((), (), s32[]{:S(2)}) async-start(), calls=%async_computation.5 | async-start | bytes 10485760 | tf_op jit(solution)/shard_map/all_gather | solution.py:67
  11.7 236.5 %copy-start.1 = (s32[512,64]{0,1:T(8,128)}, s32[512,64]{0,1:T(8,128)S(1)}, u32[]{:S(2)}) copy-start(s32[512,64]{0,1:T(8,128)S(1)} %fusion.47) | copy-start | bytes 393220
  248.2 22.0 %copy-start.3 = (bf16[1,512,2048]{2,1,0:T(8,128)(2,1)}, bf16[1,512,2048]{2,1,0:T(8,128)(2,1)S(1)}, u32[]{:S(2)}) copy-start(bf16[1,512,2048]{2,1,0:T(8,128)(2,1)S(1)} %get-tuple-element.10) | copy-start | bytes 6291460
  248.2 22.0 %copy-start.8 = (f32[512]{0:T(512)}, f32[512]{0:T(512)S(1)}, u32[]{:S(2)}) copy-start(f32[512]{0:T(512)S(1)} %add_rsqrt_fusion) | copy-start | bytes 6148
  846.1 10.1 copy-start.7
  846.1 372.6 %all-to-all-start.1 = ((bf16[16,512,2048]{2,0,1:T(8,128)(2,1)}), bf16[16,512,2048]{2,0,1:T(8,128)(2,1)}, u32[]{:S(2)}, u32[]{:S(2)}) async-start(bf16[16,512,2048]{2,0,1:T(8,128)(2,1)} %copy.78), calls=%async_computation.1 | async-start | bytes 67108864 | tf_op jit(solution)/shard_map/all_to_all | solution.py:79
  856.2 0.9 copy-start.2
  857.1 34.4 %copy-start.4 = (bf16[1,512,2048]{2,1,0:T(8,128)(2,1)S(1)}, bf16[1,512,2048]{2,1,0:T(8,128)(2,1)}, u32[]{:S(2)}) copy-start(bf16[1,512,2048]{2,1,0:T(8,128)(2,1)} %copy-done.3) | copy-start | bytes 6291460
  857.1 34.4 %copy-start.9 = (f32[512]{0:T(512)S(1)}, f32[512]{0:T(512)}, u32[]{:S(2)}) copy-start(f32[512]{0:T(512)} %copy-done.8) | copy-start | bytes 6148
Sparse Core Ops, SparseCore 0:
  8.9 58.5 all-gather.6
  69.0 55.7 all-gather.8
  126.3 55.7 all-gather.4
  183.4 55.7 all-gather.10
where the time goes:
time: 1380 us; the launch traced here: 1370 us
  waiting for transfers between devices  467 us (34%)
  blocking collectives  381 us (28%)
  local copies, waits for them, and re-layouts  248 us (18%)
  matrix products  212 us (15%)
  other arithmetic  39.1 us (3%)
  between operations  13.9 us (1%)
    all_to_all x1, blocking collectives, local_layer(): recv_rows = lax.all_to_all(send_rows, 'ep', 0, 1, tiled=True)  381 us
    all_to_all x1, waiting for transfers between devices, local_layer(): back_rows = lax.all_to_all(done_rows, 'ep', 1, 0, tiled=True)  289 us
    gather x1, local copies, waits for them, and re-layouts, combine_rows(): picked = jnp.take(table, flat_slot, axis=0)  95.9 us
    dot_general x1, matrix products, expert_ffn(): jnp.einsum('enf,efd->end', activated, w_two, preferred_element_type=jnp.f...  85.4 us
    dot_general x1, matrix products, expert_ffn(): jnp.einsum('end,edf->enf', rows, w_one, preferred_element_type=jnp.float32)  56.7 us
    all_gather x1, waiting for transfers between devices, local_layer(): full_query = lax.all_gather(w_query, 'ep', axis=0, tiled=True)  55.8 us
    all_gather x1, waiting for transfers between devices, local_layer(): full_key = lax.all_gather(w_key, 'ep', axis=0, tiled=True)  48 us
    all_gather x1, waiting for transfers between devices, local_layer(): full_out = lax.all_gather(w_out, 'ep', axis=0, tiled=True)  44.6 us
  transfers between devices with their start and end apart: 5, of which 5 were waited for; matrix products, arithmetic and copies ran while one was open for 9% of the time, Pallas kernels for 0%

commit v1 on v0

v1 whole, which is shorter than its diff:
```python
import functools
import jax
import jax.numpy as jnp
from jax import lax
from jax.experimental import pallas as pl
from jax.experimental.pallas import tpu as pltpu
from jax.sharding import PartitionSpec as P

EPS = 1e-6
PAIR = [(0, 1), (1, 0), (2, 3), (3, 2)]
ACROSS = [(0, 2), (2, 0), (1, 3), (3, 1)]
SWAP = [(0, 1), (1, 0)]
VMEM_CAP = 60 * 1024 * 1024
F32 = jnp.float32
BF16 = jnp.bfloat16


def rms_norm(vals):
    wide = vals.astype(F32)
    return wide * lax.rsqrt(jnp.mean(wide * wide, axis=-1, keepdims=True) + EPS)


def params(*semantics):
    return pltpu.CompilerParams(dimension_semantics=semantics, vmem_limit_bytes=VMEM_CAP)


def piece_sum(offs_ref, left_ref, piece_refs):
    total = None
    for idx, ref in enumerate(piece_refs):
        depth = ref.shape[0]
        cols = pl.ds(pl.multiple_of(offs_ref[idx], depth), depth)
        part = jnp.dot(left_ref[:, cols], ref[...], preferred_element_type=F32)
        total = part if total is None else total + part
    return total


def proj_kernel(offs_ref, left_ref, *refs):
    refs[-1][...] = piece_sum(offs_ref, left_ref, refs[:-1]).astype(BF16)


def project(offs, normed, pieces, block=512):
    rows, depth = normed.shape
    cols = pieces[0].shape[1]
    specs = [pl.BlockSpec((piece.shape[0], block), lambda n: (0, n)) for piece in pieces]
    return pl.pallas_call(
        proj_kernel,
        grid=(cols // block,),
        in_specs=[pl.BlockSpec(memory_space=pltpu.SMEM), pl.BlockSpec((rows, depth), lambda n: (0, 0))] + specs,
        out_specs=pl.BlockSpec((rows, block), lambda n: (0, n)),
        out_shape=jax.ShapeDtypeStruct((rows, cols), BF16),
        compiler_params=params('arbitrary'),
        cost_estimate=pl.CostEstimate(flops=2 * rows * depth * cols, bytes_accessed=2 * depth * cols, transcendentals=0),
        name='project',
    )(offs, normed, *pieces)


def attn_kernel(q_ref, k_ref, v_ref, o_ref, *, rows, scale):
    seq = q_ref.shape[0]
    for head in range(q_ref.shape[1] // 128):
        lanes = slice(head * 128, head * 128 + 128)
        for start in range(0, seq, rows):
            stop = start + rows
            scores = lax.dot_general(q_ref[start:stop, lanes], k_ref[:stop, lanes], (((1,), (1,)), ((), ())),
                                     preferred_element_type=F32) * scale
            row_id = lax.broadcasted_iota(jnp.int32, (rows, stop), 0) + start
            col_id = lax.broadcasted_iota(jnp.int32, (rows, stop), 1)
            scores = jnp.where(row_id >= col_id, scores, -jnp.inf)
            top = jnp.max(scores, axis=-1, keepdims=True)
            expo = jnp.exp(scores - top)
            weights = (expo / jnp.sum(expo, axis=-1, keepdims=True)).astype(BF16)
            o_ref[start:stop, lanes] = jnp.dot(weights, v_ref[:stop, lanes], preferred_element_type=F32).astype(BF16)


def attend(query, keys, values, head_dim, heads_step=2):
    seq, width = query.shape
    block = head_dim * heads_step
    spec = pl.BlockSpec((seq, block), lambda h: (0, h))
    return pl.pallas_call(
        functools.partial(attn_kernel, rows=128, scale=head_dim ** -0.5),
        grid=(width // block,),
        in_specs=[spec] * 3,
        out_specs=spec,
        out_shape=jax.ShapeDtypeStruct((seq, width), BF16),
        compiler_params=params('arbitrary'),
        cost_estimate=pl.CostEstimate(flops=8 * seq * seq * width, bytes_accessed=8 * seq * width, transcendentals=0),
        name='attend',
    )(query, keys, values)


def out_kernel(offs_ref, left_ref, x_ref, *refs):
    hidden = (x_ref[...].astype(F32) + piece_sum(offs_ref, left_ref, refs[:-2])).astype(BF16)
    refs[-2][...] = hidden
    refs[-1][...] = rms_norm(hidden).astype(BF16)


def out_project(offs, context, tokens, pieces, block=256):
    rows, depth = context.shape
    cols = pieces[0].shape[1]
    row_spec = pl.BlockSpec((block, cols), lambda m: (m, 0))
    return pl.pallas_call(
        out_kernel,
        grid=(rows // block,),
        in_specs=[pl.BlockSpec(memory_space=pltpu.SMEM), pl.BlockSpec((block, depth), lambda m: (m, 0)), row_spec]
        + [pl.BlockSpec(piece.shape, lambda m: (0, 0)) for piece in pieces],
        out_specs=[row_spec, row_spec],
        out_shape=[jax.ShapeDtypeStruct((rows, cols), BF16)] * 2,
        compiler_params=params('arbitrary'),
        cost_estimate=pl.CostEstimate(flops=2 * rows * depth * cols, bytes_accessed=2 * depth * cols, transcendentals=0),
        name='out_project',
    )(offs, context, tokens, *pieces)


def up_kernel(pos_lane_ref, pos_ref, gate_ref, u0_ref, u1_ref, w1_ref, w3_ref, act_ref, mix_ref, rows_ref, *, cap):
    expert = pl.program_id(0)
    seq = u0_ref.shape[0]
    slots = lax.broadcasted_iota(jnp.int32, (cap, seq), 0)
    for src, u_ref in enumerate((u0_ref, u1_ref)):
        pick = (pos_lane_ref[0, src:src + 1, :] == slots).astype(F32).astype(BF16)
        rows_ref[src * cap:(src + 1) * cap, :] = jnp.dot(pick, u_ref[...], preferred_element_type=F32).astype(BF16)
    rows = rows_ref[...]
    first = jnp.dot(rows, w1_ref[0], preferred_element_type=F32)
    third = jnp.dot(rows, w3_ref[0], preferred_element_type=F32)
    act_ref[0] = (jax.nn.silu(first) * third).astype(BF16)
    lanes = lax.broadcasted_iota(jnp.int32, (seq, pos_ref.shape[2]), 1)
    cap_lanes = lax.broadcasted_iota(jnp.int32, (seq, cap), 1)
    for src in range(2):
        place = jnp.sum(jnp.where(lanes == expert, pos_ref[src], 0), axis=-1, keepdims=True)
        gate = jnp.sum(jnp.where(lanes == expert, gate_ref[src], 0.0), axis=-1, keepdims=True)
        hit = place == cap_lanes
        rest = gate
        for term in range(3):
            part = rest.astype(BF16).astype(F32)
            mix_ref[src, :, term * cap:(term + 1) * cap] = jnp.where(hit, part, 0.0).astype(BF16)
            rest = rest - part


def expert_up(pos_lane, pos, gates, u0, u1, w_one, w_three, cap):
    count, depth, width = w_one.shape
    seq = u0.shape[0]
    whole2 = pl.BlockSpec((seq, depth), lambda e: (0, 0))
    whole3 = pl.BlockSpec((2, seq, count), lambda e: (0, 0, 0))
    w_spec = pl.BlockSpec((1, depth, width), lambda e: (e, 0, 0))
    return pl.pallas_call(
        functools.partial(up_kernel, cap=cap),
        grid=(count,),
        in_specs=[pl.BlockSpec((1, 2, seq), lambda e: (e, 0, 0)), whole3, whole3, whole2, whole2, w_spec, w_spec],
        out_specs=[pl.BlockSpec((1, 2 * cap, width), lambda e: (e, 0, 0)),
                   pl.BlockSpec((2, seq, 3 * cap), lambda e: (0, 0, e))],
        out_shape=[jax.ShapeDtypeStruct((count, 2 * cap, width), BF16),
                   jax.ShapeDtypeStruct((2, seq, count * 3 * cap), BF16)],
        scratch_shapes=[pltpu.VMEM((2 * cap, depth), BF16)],
        compiler_params=params('arbitrary'),
        cost_estimate=pl.CostEstimate(flops=8 * cap * depth * width * count + 4 * cap * seq * depth * count,
                                      bytes_accessed=4 * count * depth * width, transcendentals=0),
        name='expert_up',
    )(pos_lane, pos, gates, u0, u1, w_one, w_three)


def down_kernel(act_ref, w2_ref, mix_ref, out_ref, *, cap, per):
    @pl.when(pl.program_id(0) == 0)
    def _():
        out_ref[...] = jnp.zeros_like(out_ref)

    stack = [[], []]
    for idx in range(per):
        done = jnp.dot(act_ref[idx], w2_ref[idx], preferred_element_type=F32).astype(BF16)
        for src in range(2):
            stack[src] += [done[src * cap:(src + 1) * cap]] * 3
    for src in range(2):
        out_ref[src] += jnp.dot(mix_ref[src], jnp.concatenate(stack[src], axis=0), preferred_element_type=F32)


def expert_down(act, w_two, mix, cap, part, parts, per=2):
    count, width, model = w_two.shape
    seq = mix.shape[1]
    block = model // parts
    return pl.pallas_call(
        functools.partial(down_kernel, cap=cap, per=per),
        grid=(count // per,),
        in_specs=[pl.BlockSpec((per, 2 * cap, width), lambda e: (e, 0, 0)),
                  pl.BlockSpec((per, width, block), lambda e: (e, 0, part)),
                  pl.BlockSpec((2, seq, 3 * cap * per), lambda e: (0, 0, e))],
        out_specs=pl.BlockSpec((2, seq, block), lambda e: (0, 0, 0)),
        out_shape=jax.ShapeDtypeStruct((2, seq, block), F32),
        compiler_params=params('arbitrary'),
        cost_estimate=pl.CostEstimate(flops=(4 * cap * width * block + 12 * seq * cap * block) * count,
                                      bytes_accessed=2 * count * width * block, transcendentals=0),
        name='expert_down',
    )(act, w_two, mix)


def solution(mesh):
    tok_spec = P(('dp', 'ep'))
    row_spec = P('ep')

    def local_layer(tokens, w_query, w_key, w_value, w_out, w_router, w_one, w_three, w_two, expert_ids):
        seq, model = tokens.shape[1:]
        head_dim = w_query.shape[2]
        choices = expert_ids.shape[2]
        experts = w_router.shape[1]
        own_experts = w_one.shape[0]
        cap = 2 * seq * choices // experts
        group = lax.axis_index('dp')
        me = lax.axis_index('ep')
        x_rows = tokens[0]
        shard = w_out.shape[0]
        half = shard // 2

        pair = functools.partial(lax.ppermute, axis_name='ep', perm=PAIR)
        across = functools.partial(lax.ppermute, axis_name='ep', perm=ACROSS)
        swap = functools.partial(lax.ppermute, axis_name='dp', perm=SWAP)

        def gather(weight):
            mine = lax.dynamic_slice_in_dim(weight, group * half, half, 0).reshape(half, -1)
            full = weight.reshape(shard, -1)
            far = across(mine)
            far_other = swap(far)
            return [full, pair(full), far, far_other, pair(far), pair(far_other)]

        offs = jnp.stack([me * shard, (me ^ 1) * shard,
                          (me ^ 2) * shard + group * half, (me ^ 2) * shard + (1 - group) * half,
                          (me ^ 3) * shard + group * half, (me ^ 3) * shard + (1 - group) * half]).astype(jnp.int32)
        q_parts, k_parts, v_parts, o_parts = [gather(w) for w in (w_query, w_key, w_value, w_out)]

        ids = expert_ids[0]
        ids_pair = pair(ids)
        ids_far = across(ids)
        ids_all = jnp.stack([ids, ids_pair, ids_far, pair(ids_far)])
        mine = me * own_experts + jnp.arange(own_experts, dtype=jnp.int32)
        member = jnp.any(ids_all[:, :, :, None] == mine, axis=2)
        count = member.astype(jnp.int32)
        pos = jnp.where(member, jnp.cumsum(count, axis=1) - count, -1)
        pos_lane = pos.transpose(2, 0, 1)

        normed = rms_norm(x_rows).astype(BF16)
        query = project(offs, normed, q_parts)
        keys = project(offs, normed, k_parts)
        values = project(offs, normed, v_parts)
        context = attend(query, keys, values, head_dim)
        hidden, u_own = out_project(offs, context, x_rows, o_parts)

        u_far = across(u_own)
        u_pair = pair(u_own)
        u_far_pair = pair(u_far)

        logits = jnp.dot(rms_norm(hidden), w_router, precision=lax.Precision.HIGHEST, preferred_element_type=F32)
        chosen = jnp.any(ids[:, :, None] == jnp.arange(experts, dtype=jnp.int32), axis=1)
        gates = jax.nn.softmax(jnp.where(chosen, logits, -jnp.inf), axis=-1)
        gates_far = across(gates)
        pick = functools.partial(lax.dynamic_slice_in_dim, start_index=me * own_experts, slice_size=own_experts, axis=1)
        gates_near = jnp.stack([pick(gates), pick(pair(gates))])
        gates_away = jnp.stack([pick(gates_far), pick(pair(gates_far))])

        act_near, mix_near = expert_up(pos_lane[:, 0:2], pos[0:2], gates_near, u_own, u_pair, w_one, w_three, cap)
        act_away, mix_away = expert_up(pos_lane[:, 2:4], pos[2:4], gates_away, u_far, u_far_pair, w_one, w_three, cap)

        parts = 4
        back = []
        for part in range(parts):
            sums = expert_down(act_away, w_two, mix_away, cap, part, parts)
            back.append(across(sums[0] + pair(sums[1])))
        outs = []
        for part in range(parts):
            sums = expert_down(act_near, w_two, mix_near, cap, part, parts)
            block = model // parts
            near = hidden[:, part * block:(part + 1) * block].astype(F32) + (sums[0] + pair(sums[1]))
            outs.append((near + back[part]).astype(BF16))
        return jnp.concatenate(outs, axis=1)[None]

    return jax.shard_map(local_layer, mesh=mesh, in_specs=(tok_spec, row_spec, row_spec, row_spec, row_spec, P(), row_spec, row_spec, row_spec, tok_spec), out_specs=tok_spec, check_vma=False)
```

time: 1380 us -> 644 us (0.47)
  blocking collectives: 381 us -> 0 us
  Pallas kernels: 0 us -> 335 us
  waiting for transfers between devices: 467 us -> 232 us
  local copies, waits for them, and re-layouts: 248 us -> 30.9 us
  matrix products: 212 us -> 4.45 us
  other arithmetic: 39.1 us -> 16.2 us
  starting transfers between devices: 10.2 us -> 25 us
    all_to_all x1 -> x0, blocking collectives: 381 us -> none  [local_layer(): recv_rows = lax.all_to_all(send_rows, 'ep', 0, 1, tiled=True)]
    pallas_call x0 -> x15, Pallas kernels: none -> 335 us  [the longest x8 153 us: expert_down(): pl.pallas_call(functools.partial(down_kernel, cap=cap, per=per), grid=(co...]
    all_to_all x1 -> x0, waiting for transfers between devices: 289 us -> none  [local_layer(): back_rows = lax.all_to_all(done_rows, 'ep', 1, 0, tiled=True)]
    ppermute x0 -> x41, waiting for transfers between devices: none -> 232 us  [the longest x8 88.5 us: local_layer(): back.append(across(sums[0] + pair(sums[1])))]
    dot_general x8 -> x1, matrix products: 212 us -> 4.45 us  [local_layer(): jnp.dot(rms_norm(hidden), w_router, precision=lax.Precision.HIGHEST, pref...]
    all_gather x4 -> x0, waiting for transfers between devices: 176 us -> none  [the longest x1 55.8 us: local_layer(): full_query = lax.all_gather(w_query, 'ep', axis=0, tiled=True)]
    gather x13 -> x0, local copies, waits for them, and re-layouts: 163 us -> none  [the longest x1 95.9 us: combine_rows(): picked = jnp.take(table, flat_slot, axis=0)]
    all_to_all x2 -> x0, local copies, waits for them, and re-layouts: 53 us -> none  [the longest x1 30.1 us: local_layer(): back_rows = lax.all_to_all(done_rows, 'ep', 1, 0, tiled=True)]
  transfers between devices with their start and end apart: 5 -> 41, of which waited for: 5 -> 14; matrix products, arithmetic and copies ran while one was open for 9% -> 6% of each run, Pallas kernels for 0% -> 50%
where the time goes in v1:
time: 644 us
  Pallas kernels  335 us (52%)
  waiting for transfers between devices  232 us (36%)
  local copies, waits for them, and re-layouts  30.9 us (5%)
  starting transfers between devices  25 us (4%)
  other arithmetic  16.2 us (3%)
    pallas_call x8, Pallas kernels, expert_down(): pl.pallas_call(functools.partial(down_kernel, cap=cap, per=per), grid=(co...  153 us
    pallas_call x2, Pallas kernels, expert_up(): pl.pallas_call(functools.partial(up_kernel, cap=cap), grid=(count,), in_s...  122 us
    ppermute x8, waiting for transfers between devices, local_layer(): back.append(across(sums[0] + pair(sums[1])))  88.5 us
    ppermute x4, waiting for transfers between devices, gather(): far_other = swap(far)  56.4 us
    ppermute x1, waiting for transfers between devices, local_layer(): ids_far = across(ids)  42.4 us
    ppermute x4, waiting for transfers between devices, gather(): far = across(mine)  40.4 us
    pallas_call x3, Pallas kernels, project(): pl.pallas_call(proj_kernel, grid=(cols // block,), in_specs=[pl.BlockSpec...  27.2 us
    pallas_call x1, Pallas kernels, attend(): pl.pallas_call(functools.partial(attn_kernel, rows=128, scale=head_dim **...  22.3 us
  transfers between devices with their start and end apart: 41, of which 14 were waited for; matrix products, arithmetic and copies ran while one was open for 6% of the time, Pallas kernels for 50%

profile of v1, /device:TPU:0, one launch (start us, length us, event | category | flops | bytes accessed | tf_op | source)
XLA Modules:
  0.0 643.7 jit_solution(10714415452387932920)
XLA Ops:
  1.5 3.4 collective-permute-start.16
  6.3 1.5 collective-permute-start.6
  8.8 20.0 %collective-permute-done.16.refs_2_ = bf16[256,2048]{1,0:T(8,128)(2,1)S(1)} collective-permute-done((bf16[256,2048]{1,0:T(8,128)(2,1)S(1)}, bf16[256,2048]{1,0:T(8,128)(2,1)S(1)}, u32[]{:S(2)}, u32[]{:S(2)}) %collective-permute-start.16) | collective-permute-done | bytes 1048608 | tf_op jit(solution)/shard_map/ppermute | solution.py:216
  28.8 2.0 collective-permute-start.17
  30.9 20.4 %collective-permute-done.11.refs_2_ = bf16[256,2048]{1,0:T(8,128)(2,1)} collective-permute-done((bf16[256,2048]{1,0:T(8,128)(2,1)S(1)}, bf16[256,2048]{1,0:T(8,128)(2,1)}, u32[]{:S(2)}, u32[]{:S(2)}) %collective-permute-start.11) | collective-permute-done | bytes 1048608 | tf_op jit(solution)/shard_map/ppermute | solution.py:216
  51.3 2.0 collective-permute-start.21
  53.3 42.4 %collective-permute-done.21 = s32[512,8]{0,1:T(8,128)S(1)} collective-permute-done((s32[512,8]{0,1:T(8,128)S(1)}, s32[512,8]{0,1:T(8,128)S(1)}, u32[]{:S(2)}, u32[]{:S(2)}) %collective-permute-start.21) | collective-permute-done | bytes 16416 | tf_op jit(solution)/shard_map/ppermute | solution.py:227
  98.1 1.8 collective-permute-start.12
  99.9 2.0 copy.62
  103.6 1.8 collective-permute-start.2
  105.4 1.9 copy.60
  107.3 1.9 copy.61
  109.7 14.5 %collective-permute-done.12.refs_3_ = bf16[256,2048]{1,0:T(8,128)(2,1)} collective-permute-done((bf16[256,2048]{1,0:T(8,128)(2,1)}, bf16[256,2048]{1,0:T(8,128)(2,1)}, u32[]{:S(2)}, u32[]{:S(2)}) %collective-permute-start.12) | collective-permute-done | bytes 1048608 | tf_op jit(solution)/shard_map/ppermute | solution.py:217
  124.7 1.7 fusion.1.left_ref
  126.4 20.2 %collective-permute-done.7.refs_3_ = bf16[256,2048]{1,0:T(8,128)(2,1)} collective-permute-done((bf16[256,2048]{1,0:T(8,128)(2,1)}, bf16[256,2048]{1,0:T(8,128)(2,1)}, u32[]{:S(2)}, u32[]{:S(2)}) %collective-permute-start.7) | collective-permute-done | bytes 1048608 | tf_op jit(solution)/shard_map/ppermute | solution.py:217
  146.6 21.7 %collective-permute-done.2.refs_3_ = bf16[256,2048]{1,0:T(8,128)(2,1)} collective-permute-done((bf16[256,2048]{1,0:T(8,128)(2,1)}, bf16[256,2048]{1,0:T(8,128)(2,1)}, u32[]{:S(2)}, u32[]{:S(2)}) %collective-permute-start.2) | collective-permute-done | bytes 1048608 | tf_op jit(solution)/shard_map/ppermute | solution.py:217
  170.2 4.7 reduce-window.6
  178.2 9.1 %project.3.q_ref = bf16[512,2048]{1,0:T(8,128)(2,1)} custom-call(s32[6]{0:T(128)} %stack.57.offs_ref, bf16[512,2048]{1,0:T(8,128)(2,1)} %fusion.1.left_ref, bf16[512,2048]{1,0:T(8,128)(2,1)} %bitcast.132.refs_0_, bf16[512,2048]{1,0:T(8,128)(2,1)} %collective-permute-done.refs_1_, bf16[256,2048]{1,0:T(8,128)(2,1)} %collective-permute-done.1.refs_2_, ...), custom_call_target="tpu_custom_call" | custom-call | flops 4294967296 | bytes 8388608 | tf_op jit(solution)/shard_map/project/pallas_call | solution.py:45
  187.9 9.0 %project.4.k_ref = bf16[512,2048]{1,0:T(8,128)(2,1)} custom-call(s32[6]{0:T(128)} %stack.57.offs_ref, bf16[512,2048]{1,0:T(8,128)(2,1)} %fusion.1.left_ref, bf16[512,2048]{1,0:T(8,128)(2,1)} %bitcast.131.refs_0_, bf16[512,2048]{1,0:T(8,128)(2,1)} %collective-permute-done.5.refs_1_, bf16[256,2048]{1,0:T(8,128)(2,1)} %collective-permute-done.6.refs_2_, ...), custom_call_target="tpu_custom_call" | custom-call | flops 4294967296 | bytes 8388608 | tf_op jit(solution)/shard_map/project/pallas_call | solution.py:45
  196.9 9.0 %project.5.v_ref = bf16[512,2048]{1,0:T(8,128)(2,1)} custom-call(s32[6]{0:T(128)} %stack.57.offs_ref, bf16[512,2048]{1,0:T(8,128)(2,1)} %fusion.1.left_ref, bf16[512,2048]{1,0:T(8,128)(2,1)} %bitcast.130.refs_0_, bf16[512,2048]{1,0:T(8,128)(2,1)} %collective-permute-done.10.refs_1_, bf16[256,2048]{1,0:T(8,128)(2,1)} %collective-permute-done.11.refs_2_, ...), custom_call_target="tpu_custom_call" | custom-call | flops 4294967296 | bytes 8388608 | tf_op jit(solution)/shard_map/project/pallas_call | solution.py:45
  205.9 22.3 %attend.1.left_ref = bf16[512,2048]{1,0:T(8,128)(2,1)} custom-call(bf16[512,2048]{1,0:T(8,128)(2,1)} %project.3.q_ref, bf16[512,2048]{1,0:T(8,128)(2,1)} %project.4.k_ref, bf16[512,2048]{1,0:T(8,128)(2,1)} %project.5.v_ref), custom_call_target="tpu_custom_call" | custom-call | flops 4294967296 | bytes 8388608 | tf_op jit(solution)/shard_map/attend/pallas_call | solution.py:78
  228.2 10.5 %out_project.1 = (bf16[512,2048]{1,0:T(8,128)(2,1)}, bf16[512,2048]{1,0:T(8,128)(2,1)}) custom-call(s32[6]{0:T(128)} %stack.57.offs_ref, bf16[512,2048]{1,0:T(8,128)(2,1)} %attend.1.left_ref, bf16[512,2048]{1,0:T(8,128)(2,1)} %bitcast.136, bf16[512,2048]{1,0:T(8,128)(2,1)} %refs_0_.1, bf16[512,2048]{1,0:T(8,128)(2,1)} %collective-permute-done.15.refs_1_, ...), custom_call_target="tpu_custom_call" | custom-call | flops 4294967296 | bytes 8388608 | tf_op jit(solution)/shard_map/out_project/pallas_call | solution.py:100
  241.2 4.5 fusion.33
  245.7 1.7 collective-permute-start.26
  249.5 1.5 collective-permute-done.26
  253.3 61.2 %expert_up.2 = (bf16[16,256,1024]{2,1,0:T(8,128)(2,1)}, bf16[2,512,6144]{2,1,0:T(8,128)(2,1)}) custom-call(s32[16,2,512]{2,1,0:T(2,128)} %copy.44.pos_lane_ref, s32[2,512,16]{2,1,0:T(8,128)} %get-tuple-element.21.pos_ref, f32[2,512,16]{2,1,0:T(8,128)} %copy.45.gate_ref, bf16[512,2048]{1,0:T(8,128)(2,1)} %get-tuple-element.12.u0_ref, ...), custom_call_target="tpu_custom_call" | custom-call | flops 42949672960 | bytes 134217728 | tf_op jit(solution)/shard_map/expert_up/pallas_call | solution.py:143
  314.5 19.1 %expert_down.14 = f32[2,512,512]{2,1,0:T(8,128)} custom-call(bf16[16,256,1024]{2,1,0:T(8,128)(2,1)} %get-tuple-element.13.act_ref, bf16[16,1024,2048]{2,1,0:T(8,128)(2,1)} %w2_ref.15, bf16[2,512,6144]{2,1,0:T(8,128)(2,1)} %get-tuple-element.14.mix_ref), custom_call_target="tpu_custom_call" | custom-call | flops 10737418240 | bytes 16777216 | tf_op jit(solution)/shard_map/expert_down/pallas_call | solution.py:177
  333.7 2.3 slice_bitcast_fusion.2
  336.2 19.0 %expert_down.12 = f32[2,512,512]{2,1,0:T(8,128)} custom-call(bf16[16,256,1024]{2,1,0:T(8,128)(2,1)} %get-tuple-element.13.act_ref, bf16[16,1024,2048]{2,1,0:T(8,128)(2,1)} %w2_ref.15, bf16[2,512,6144]{2,1,0:T(8,128)(2,1)} %get-tuple-element.14.mix_ref), custom_call_target="tpu_custom_call" | custom-call | flops 10737418240 | bytes 16777216 | tf_op jit(solution)/shard_map/expert_down/pallas_call | solution.py:177
  355.2 2.3 slice_bitcast_fusion.6
  357.8 19.1 %expert_down.8 = f32[2,512,512]{2,1,0:T(8,128)} custom-call(bf16[16,256,1024]{2,1,0:T(8,128)(2,1)} %get-tuple-element.13.act_ref, bf16[16,1024,2048]{2,1,0:T(8,128)(2,1)} %w2_ref.15, bf16[2,512,6144]{2,1,0:T(8,128)(2,1)} %get-tuple-element.14.mix_ref), custom_call_target="tpu_custom_call" | custom-call | flops 10737418240 | bytes 16777216 | tf_op jit(solution)/shard_map/expert_down/pallas_call | solution.py:177
  376.9 2.3 slice_bitcast_fusion.14
  379.2 19.1 %expert_down.10 = f32[2,512,512]{2,1,0:T(8,128)} custom-call(bf16[16,256,1024]{2,1,0:T(8,128)(2,1)} %get-tuple-element.13.act_ref, bf16[16,1024,2048]{2,1,0:T(8,128)(2,1)} %w2_ref.15, bf16[2,512,6144]{2,1,0:T(8,128)(2,1)} %get-tuple-element.14.mix_ref), custom_call_target="tpu_custom_call" | custom-call | flops 10737418240 | bytes 16777216 | tf_op jit(solution)/shard_map/expert_down/pallas_call | solution.py:177
  399.6 60.9 %expert_up.3 = (bf16[16,256,1024]{2,1,0:T(8,128)(2,1)}, bf16[2,512,6144]{2,1,0:T(8,128)(2,1)}) custom-call(s32[16,2,512]{2,1,0:T(2,128)} %copy.46.pos_lane_ref, s32[2,512,16]{2,1,0:T(8,128)} %get-tuple-element.22.pos_ref, f32[2,512,16]{2,1,0:T(8,128)} %copy.47.gate_ref, bf16[512,2048]{1,0:T(8,128)(2,1)} %collective-permute-done.28.u0_ref, ...), custom_call_target="tpu_custom_call" | custom-call | flops 42949672960 | bytes 134217728 | tf_op jit(solution)/shard_map/expert_up/pallas_call | solution.py:143
  460.5 19.0 %expert_down.15 = f32[2,512,512]{2,1,0:T(8,128)} custom-call(bf16[16,256,1024]{2,1,0:T(8,128)(2,1)} %get-tuple-element.15.act_ref, bf16[16,1024,2048]{2,1,0:T(8,128)(2,1)} %w2_ref.15, bf16[2,512,6144]{2,1,0:T(8,128)(2,1)} %get-tuple-element.16.mix_ref), custom_call_target="tpu_custom_call" | custom-call | flops 10737418240 | bytes 16777216 | tf_op jit(solution)/shard_map/expert_down/pallas_call | solution.py:177
  479.6 19.1 %expert_down.13 = f32[2,512,512]{2,1,0:T(8,128)} custom-call(bf16[16,256,1024]{2,1,0:T(8,128)(2,1)} %get-tuple-element.15.act_ref, bf16[16,1024,2048]{2,1,0:T(8,128)(2,1)} %w2_ref.15, bf16[2,512,6144]{2,1,0:T(8,128)(2,1)} %get-tuple-element.16.mix_ref), custom_call_target="tpu_custom_call" | custom-call | flops 10737418240 | bytes 16777216 | tf_op jit(solution)/shard_map/expert_down/pallas_call | solution.py:177
  498.6 19.2 %expert_down.11 = f32[2,512,512]{2,1,0:T(8,128)} custom-call(bf16[16,256,1024]{2,1,0:T(8,128)(2,1)} %get-tuple-element.15.act_ref, bf16[16,1024,2048]{2,1,0:T(8,128)(2,1)} %w2_ref.15, bf16[2,512,6144]{2,1,0:T(8,128)(2,1)} %get-tuple-element.16.mix_ref), custom_call_target="tpu_custom_call" | custom-call | flops 10737418240 | bytes 16777216 | tf_op jit(solution)/shard_map/expert_down/pallas_call | solution.py:177
  521.1 19.2 %expert_down.9 = f32[2,512,512]{2,1,0:T(8,128)} custom-call(bf16[16,256,1024]{2,1,0:T(8,128)(2,1)} %get-tuple-element.15.act_ref, bf16[16,1024,2048]{2,1,0:T(8,128)(2,1)} %w2_ref.15, bf16[2,512,6144]{2,1,0:T(8,128)(2,1)} %get-tuple-element.16.mix_ref), custom_call_target="tpu_custom_call" | custom-call | flops 10737418240 | bytes 16777216 | tf_op jit(solution)/shard_map/expert_down/pallas_call | solution.py:177
  540.7 1.5 slice_bitcast_fusion.12
  544.0 1.6 fusion.11
  546.2 1.9 collective-permute-start.40
  548.5 1.9 collective-permute-start.34
  550.5 21.7 %collective-permute-done.40 = f32[512,512]{1,0:T(8,128)S(1)} collective-permute-done((f32[512,512]{1,0:T(8,128)S(1)}, f32[512,512]{1,0:T(8,128)S(1)}, u32[]{:S(2)}, u32[]{:S(2)}) %collective-permute-start.40) | collective-permute-done | bytes 1048608 | tf_op jit(solution)/shard_map/ppermute | solution.py:261
  572.2 22.5 %collective-permute-done.37 = f32[512,512]{1,0:T(8,128)S(1)} collective-permute-done((f32[512,512]{1,0:T(8,128)S(1)}, f32[512,512]{1,0:T(8,128)S(1)}, u32[]{:S(2)}, u32[]{:S(2)}) %collective-permute-start.37) | collective-permute-done | bytes 1048608 | tf_op jit(solution)/shard_map/ppermute | solution.py:261
  594.7 22.5 %collective-permute-done.34 = f32[512,512]{1,0:T(8,128)S(1)} collective-permute-done((f32[512,512]{1,0:T(8,128)S(1)}, f32[512,512]{1,0:T(8,128)S(1)}, u32[]{:S(2)}, u32[]{:S(2)}) %collective-permute-start.34) | collective-permute-done | bytes 1048608 | tf_op jit(solution)/shard_map/ppermute | solution.py:261
  617.2 21.9 %collective-permute-done.31 = f32[512,512]{1,0:T(8,128)S(1)} collective-permute-done((f32[512,512]{1,0:T(8,128)S(1)}, f32[512,512]{1,0:T(8,128)S(1)}, u32[]{:S(2)}, u32[]{:S(2)}) %collective-permute-start.31) | collective-permute-done | bytes 1048608 | tf_op jit(solution)/shard_map/ppermute | solution.py:261
  639.0 3.1 fusion.25
  642.1 1.6 maximum_bitcast_fusion
  (165 shorter events, 29.9 us)
Async XLA Ops:
  0.0 241.2 %copy-start = (f32[2048,64]{0,1:T(8,128)S(1)}, f32[2048,64]{0,1:T(8,128)}, u32[]{:S(2)}) copy-start(f32[2048,64]{0,1:T(8,128)} %param.15) | copy-start | bytes 1572868
  1.5 27.4 %collective-permute-start.16 = (bf16[256,2048]{1,0:T(8,128)(2,1)S(1)}, bf16[256,2048]{1,0:T(8,128)(2,1)S(1)}, u32[]{:S(2)}, u32[]{:S(2)}) collective-permute-start(bf16[256,2048]{1,0:T(8,128)(2,1)S(1)} %constant_dynamic-slice_fusion), channel_id=1, source_target_pairs={{0,2},{2,0},{1,3},{3,1},{4,6},{6,4},{5,7},{7,5}} | collective-permute-start | bytes 3145736 | tf_op jit(solution)/shard_map/ppermute | solution.py:216
  5.3 46.0 %collective-permute-start.11 = (bf16[256,2048]{1,0:T(8,128)(2,1)S(1)}, bf16[256,2048]{1,0:T(8,128)(2,1)}, u32[]{:S(2)}, u32[]{:S(2)}) collective-permute-start(bf16[256,2048]{1,0:T(8,128)(2,1)S(1)} %bitcast.146), channel_id=1, source_target_pairs={{0,2},{2,0},{1,3},{3,1},{4,6},{6,4},{5,7},{7,5}} | collective-permute-start | bytes 3145736 | tf_op jit(solution)/shard_map/ppermute | solution.py:216
  6.3 45.0 %copy-start.22 = (s32[1,512,8]{1,2,0:T(8,128)S(1)}, s32[1,512,8]{1,2,0:T(8,128)}, u32[]{:S(2)}) copy-start(s32[1,512,8]{1,2,0:T(8,128)} %param.19) | copy-start | bytes 49156
  6.3 93.6 %collective-permute-start.6 = (bf16[256,2048]{1,0:T(8,128)(2,1)S(1)}, bf16[256,2048]{1,0:T(8,128)(2,1)}, u32[]{:S(2)}, u32[]{:S(2)}) collective-permute-start(bf16[256,2048]{1,0:T(8,128)(2,1)S(1)} %bitcast.145), channel_id=1, source_target_pairs={{0,2},{2,0},{1,3},{3,1},{4,6},{6,4},{5,7},{7,5}} | collective-permute-start | bytes 3145736 | tf_op jit(solution)/shard_map/ppermute | solution.py:216
  8.3 93.5 %collective-permute-start.1 = (bf16[256,2048]{1,0:T(8,128)(2,1)S(1)}, bf16[256,2048]{1,0:T(8,128)(2,1)}, u32[]{:S(2)}, u32[]{:S(2)}) collective-permute-start(bf16[256,2048]{1,0:T(8,128)(2,1)S(1)} %bitcast.144), channel_id=1, source_target_pairs={{0,2},{2,0},{1,3},{3,1},{4,6},{6,4},{5,7},{7,5}} | collective-permute-start | bytes 3145736 | tf_op jit(solution)/shard_map/ppermute | solution.py:216
  28.8 73.0 %copy-start.24 = (bf16[256,2048]{1,0:T(8,128)(2,1)}, bf16[256,2048]{1,0:T(8,128)(2,1)S(1)}, u32[]{:S(2)}) copy-start(bf16[256,2048]{1,0:T(8,128)(2,1)S(1)} %collective-permute-done.16.refs_2_) | copy-start | bytes 3145732
  28.8 73.5 %collective-permute-start.17 = (bf16[256,2048]{1,0:T(8,128)(2,1)S(1)}, bf16[256,2048]{1,0:T(8,128)(2,1)S(1)}, u32[]{:S(2)}, u32[]{:S(2)}) collective-permute-start(bf16[256,2048]{1,0:T(8,128)(2,1)S(1)} %collective-permute-done.16.refs_2_), channel_id=1, source_target_pairs={{0,4},{4,0},{1,5},{5,1},{2,6},{6,2},{3,7},{7,3}} | collective-permute-start | bytes 3145736 | tf_op jit(solution)/shard_map/ppermute | solution.py:217
  51.3 52.3 %collective-permute-start.13 = (bf16[256,2048]{1,0:T(8,128)(2,1)}, bf16[256,2048]{1,0:T(8,128)(2,1)}, u32[]{:S(2)}, u32[]{:S(2)}) collective-permute-start(bf16[256,2048]{1,0:T(8,128)(2,1)} %collective-permute-done.11.refs_2_), channel_id=1, source_target_pairs={{0,1},{1,0},{2,3},{3,2},{4,5},{5,4},{6,7},{7,6}} | collective-permute-start | bytes 3145736 | tf_op jit(solution)/shard_map/ppermute | solution.py:218
  51.3 44.4 %collective-permute-start.21 = (s32[512,8]{0,1:T(8,128)S(1)}, s32[512,8]{0,1:T(8,128)S(1)}, u32[]{:S(2)}, u32[]{:S(2)}) collective-permute-start(s32[512,8]{0,1:T(8,128)S(1)} %bitcast.147), channel_id=1, source_target_pairs={{0,2},{2,0},{1,3},{3,1},{4,6},{6,4},{5,7},{7,5}} | collective-permute-start | bytes 49160 | tf_op jit(solution)/shard_map/ppermute | solution.py:227
  95.7 1.2 collective-permute-start.20
  96.9 1.2 collective-permute-start.22
  98.1 26.0 %collective-permute-start.12 = (bf16[256,2048]{1,0:T(8,128)(2,1)}, bf16[256,2048]{1,0:T(8,128)(2,1)}, u32[]{:S(2)}, u32[]{:S(2)}) collective-permute-start(bf16[256,2048]{1,0:T(8,128)(2,1)} %collective-permute-done.11.refs_2_), channel_id=1, source_target_pairs={{0,4},{4,0},{1,5},{5,1},{2,6},{6,2},{3,7},{7,3}} | collective-permute-start | bytes 3145736 | tf_op jit(solution)/shard_map/ppermute | solution.py:217
  99.9 24.3 %collective-permute-start.8 = (bf16[256,2048]{1,0:T(8,128)(2,1)}, bf16[256,2048]{1,0:T(8,128)(2,1)}, u32[]{:S(2)}, u32[]{:S(2)}) collective-permute-start(bf16[256,2048]{1,0:T(8,128)(2,1)} %collective-permute-done.6.refs_2_), channel_id=1, source_target_pairs={{0,1},{1,0},{2,3},{3,2},{4,5},{5,4},{6,7},{7,6}} | collective-permute-start | bytes 3145736 | tf_op jit(solution)/shard_map/ppermute | solution.py:218
  101.9 74.5 %collective-permute-start = (bf16[512,2048]{1,0:T(8,128)(2,1)}, bf16[512,2048]{1,0:T(8,128)(2,1)}, u32[]{:S(2)}, u32[]{:S(2)}) collective-permute-start(bf16[512,2048]{1,0:T(8,128)(2,1)} %bitcast.132.refs_0_), channel_id=1, source_target_pairs={{0,1},{1,0},{2,3},{3,2},{4,5},{5,4},{6,7},{7,6}} | collective-permute-start | bytes 6291464 | tf_op jit(solution)/shard_map/ppermute | solution.py:218
  103.4 43.3 %collective-permute-start.7 = (bf16[256,2048]{1,0:T(8,128)(2,1)}, bf16[256,2048]{1,0:T(8,128)(2,1)}, u32[]{:S(2)}, u32[]{:S(2)}) collective-permute-start(bf16[256,2048]{1,0:T(8,128)(2,1)} %collective-permute-done.6.refs_2_), channel_id=1, source_target_pairs={{0,4},{4,0},{1,5},{5,1},{2,6},{6,2},{3,7},{7,3}} | collective-permute-start | bytes 3145736 | tf_op jit(solution)/shard_map/ppermute | solution.py:217
  103.6 64.7 %collective-permute-start.2 = (bf16[256,2048]{1,0:T(8,128)(2,1)}, bf16[256,2048]{1,0:T(8,128)(2,1)}, u32[]{:S(2)}, u32[]{:S(2)}) collective-permute-start(bf16[256,2048]{1,0:T(8,128)(2,1)} %collective-permute-done.1.refs_2_), channel_id=1, source_target_pairs={{0,4},{4,0},{1,5},{5,1},{2,6},{6,2},{3,7},{7,3}} | collective-permute-start | bytes 3145736 | tf_op jit(solution)/shard_map/ppermute | solution.py:217
  124.2 63.2 %collective-permute-start.5 = (bf16[512,2048]{1,0:T(8,128)(2,1)}, bf16[512,2048]{1,0:T(8,128)(2,1)}, u32[]{:S(2)}, u32[]{:S(2)}) collective-permute-start(bf16[512,2048]{1,0:T(8,128)(2,1)} %bitcast.131.refs_0_), channel_id=1, source_target_pairs={{0,1},{1,0},{2,3},{3,2},{4,5},{5,4},{6,7},{7,6}} | collective-permute-start | bytes 6291464 | tf_op jit(solution)/shard_map/ppermute | solution.py:218
  124.2 51.2 %collective-permute-start.3 = (bf16[256,2048]{1,0:T(8,128)(2,1)}, bf16[256,2048]{1,0:T(8,128)(2,1)}, u32[]{:S(2)}, u32[]{:S(2)}) collective-permute-start(bf16[256,2048]{1,0:T(8,128)(2,1)} %collective-permute-done.1.refs_2_), channel_id=1, source_target_pairs={{0,1},{1,0},{2,3},{3,2},{4,5},{5,4},{6,7},{7,6}} | collective-permute-start | bytes 3145736 | tf_op jit(solution)/shard_map/ppermute | solution.py:218
  146.6 50.3 %collective-permute-start.10 = (bf16[512,2048]{1,0:T(8,128)(2,1)}, bf16[512,2048]{1,0:T(8,128)(2,1)}, u32[]{:S(2)}, u32[]{:S(2)}) collective-permute-start(bf16[512,2048]{1,0:T(8,128)(2,1)} %bitcast.130.refs_0_), channel_id=1, source_target_pairs={{0,1},{1,0},{2,3},{3,2},{4,5},{5,4},{6,7},{7,6}} | collective-permute-start | bytes 6291464 | tf_op jit(solution)/shard_map/ppermute | solution.py:218
  168.3 8.2 %collective-permute-start.4 = (bf16[256,2048]{1,0:T(8,128)(2,1)}, bf16[256,2048]{1,0:T(8,128)(2,1)}, u32[]{:S(2)}, u32[]{:S(2)}) collective-permute-start(bf16[256,2048]{1,0:T(8,128)(2,1)} %collective-permute-done.2.refs_3_), channel_id=1, source_target_pairs={{0,1},{1,0},{2,3},{3,2},{4,5},{5,4},{6,7},{7,6}} | collective-permute-start | bytes 3145736 | tf_op jit(solution)/shard_map/ppermute | solution.py:218
  175.4 12.0 %collective-permute-start.9 = (bf16[256,2048]{1,0:T(8,128)(2,1)}, bf16[256,2048]{1,0:T(8,128)(2,1)}, u32[]{:S(2)}, u32[]{:S(2)}) collective-permute-start(bf16[256,2048]{1,0:T(8,128)(2,1)} %collective-permute-done.7.refs_3_), channel_id=1, source_target_pairs={{0,1},{1,0},{2,3},{3,2},{4,5},{5,4},{6,7},{7,6}} | collective-permute-start | bytes 3145736 | tf_op jit(solution)/shard_map/ppermute | solution.py:218
  176.4 51.9 %collective-permute-start.15 = (bf16[512,2048]{1,0:T(8,128)(2,1)}, bf16[512,2048]{1,0:T(8,128)(2,1)}, u32[]{:S(2)}, u32[]{:S(2)}) collective-permute-start(bf16[512,2048]{1,0:T(8,128)(2,1)} %refs_0_.1), channel_id=1, source_target_pairs={{0,1},{1,0},{2,3},{3,2},{4,5},{5,4},{6,7},{7,6}} | collective-permute-start | bytes 6291464 | tf_op jit(solution)/shard_map/ppermute | solution.py:218
  176.6 20.4 %collective-permute-start.14 = (bf16[256,2048]{1,0:T(8,128)(2,1)}, bf16[256,2048]{1,0:T(8,128)(2,1)}, u32[]{:S(2)}, u32[]{:S(2)}) collective-permute-start(bf16[256,2048]{1,0:T(8,128)(2,1)} %collective-permute-done.12.refs_3_), channel_id=1, source_target_pairs={{0,1},{1,0},{2,3},{3,2},{4,5},{5,4},{6,7},{7,6}} | collective-permute-start | bytes 3145736 | tf_op jit(solution)/shard_map/ppermute | solution.py:218
  187.3 40.9 %collective-permute-start.18 = (bf16[256,2048]{1,0:T(8,128)(2,1)S(1)}, bf16[256,2048]{1,0:T(8,128)(2,1)}, u32[]{:S(2)}, u32[]{:S(2)}) collective-permute-start(bf16[256,2048]{1,0:T(8,128)(2,1)S(1)} %copy-done.25), channel_id=1, source_target_pairs={{0,1},{1,0},{2,3},{3,2},{4,5},{5,4},{6,7},{7,6}} | collective-permute-start | bytes 3145736 | tf_op jit(solution)/shard_map/ppermute | solution.py:218
  187.4 40.8 %collective-permute-start.19 = (bf16[256,2048]{1,0:T(8,128)(2,1)S(1)}, bf16[256,2048]{1,0:T(8,128)(2,1)}, u32[]{:S(2)}, u32[]{:S(2)}) collective-permute-start(bf16[256,2048]{1,0:T(8,128)(2,1)S(1)} %copy-done.27), channel_id=1, source_target_pairs={{0,1},{1,0},{2,3},{3,2},{4,5},{5,4},{6,7},{7,6}} | collective-permute-start | bytes 3145736 | tf_op jit(solution)/shard_map/ppermute | solution.py:218
  238.7 14.6 %collective-permute-start.24 = (bf16[512,2048]{1,0:T(8,128)(2,1)}, bf16[512,2048]{1,0:T(8,128)(2,1)}, u32[]{:S(2)}, u32[]{:S(2)}) collective-permute-start(bf16[512,2048]{1,0:T(8,128)(2,1)} %get-tuple-element.12.u0_ref), channel_id=1, source_target_pairs={{0,1},{1,0},{2,3},{3,2},{4,5},{5,4},{6,7},{7,6}} | collective-permute-start | bytes 6291464 | tf_op jit(solution)/shard_map/ppermute | solution.py:243
  245.7 5.2 collective-permute-start.26
  247.5 3.5 collective-permute-start.23
  249.1 108.4 %collective-permute-start.28 = (bf16[512,2048]{1,0:T(8,128)(2,1)}, bf16[512,2048]{1,0:T(8,128)(2,1)}, u32[]{:S(2)}, u32[]{:S(2)}) collective-permute-start(bf16[512,2048]{1,0:T(8,128)(2,1)} %get-tuple-element.12.u0_ref), channel_id=1, source_target_pairs={{0,2},{2,0},{1,3},{3,1},{4,6},{6,4},{5,7},{7,5}} | collective-permute-start | bytes 6291464 | tf_op jit(solution)/shard_map/ppermute | solution.py:242
  251.0 1.3 collective-permute-start.27
  336.0 212.3 %collective-permute-start.38 = (f32[512,512]{1,0:T(8,128)}, f32[512,512]{1,0:T(8,128)}, u32[]{:S(2)}, u32[]{:S(2)}) collective-permute-start(f32[512,512]{1,0:T(8,128)} %slice_bitcast_fusion.2), channel_id=1, source_target_pairs={{0,1},{1,0},{2,3},{3,2},{4,5},{5,4},{6,7},{7,6}} | collective-permute-start | bytes 3145736 | tf_op jit(solution)/shard_map/ppermute | solution.py:266
  357.5 40.8 %collective-permute-start.29 = (bf16[512,2048]{1,0:T(8,128)(2,1)}, bf16[512,2048]{1,0:T(8,128)(2,1)S(1)}, u32[]{:S(2)}, u32[]{:S(2)}) collective-permute-start(bf16[512,2048]{1,0:T(8,128)(2,1)} %collective-permute-done.28.u0_ref), channel_id=1, source_target_pairs={{0,1},{1,0},{2,3},{3,2},{4,5},{5,4},{6,7},{7,6}} | collective-permute-start | bytes 6291464 | tf_op jit(solution)/shard_map/ppermute | solution.py:244
  518.9 23.5 %collective-permute-start.39 = (f32[512,512]{1,0:T(8,128)}, f32[512,512]{1,0:T(8,128)S(1)}, u32[]{:S(2)}, u32[]{:S(2)}) collective-permute-start(f32[512,512]{1,0:T(8,128)} %slice_bitcast_fusion), channel_id=1, source_target_pairs={{0,1},{1,0},{2,3},{3,2},{4,5},{5,4},{6,7},{7,6}} | collective-permute-start | bytes 3145736 | tf_op jit(solution)/shard_map/ppermute | solution.py:261
  520.9 22.0 %collective-permute-start.36 = (f32[512,512]{1,0:T(8,128)}, f32[512,512]{1,0:T(8,128)}, u32[]{:S(2)}, u32[]{:S(2)}) collective-permute-start(f32[512,512]{1,0:T(8,128)} %slice_bitcast_fusion.4), channel_id=1, source_target_pairs={{0,1},{1,0},{2,3},{3,2},{4,5},{5,4},{6,7},{7,6}} | collective-permute-start | bytes 3145736 | tf_op jit(solution)/shard_map/ppermute | solution.py:261
  540.3 5.3 collective-permute-start.33
  542.2 3.9 collective-permute-start.30
  542.4 6.0 collective-permute-start.35
  542.9 7.5 %collective-permute-start.32 = (f32[512,512]{1,0:T(8,128)S(1)}, f32[512,512]{1,0:T(8,128)S(1)}, u32[]{:S(2)}, u32[]{:S(2)}) collective-permute-start(f32[512,512]{1,0:T(8,128)S(1)} %slice_bitcast_fusion.10), channel_id=1, source_target_pairs={{0,1},{1,0},{2,3},{3,2},{4,5},{5,4},{6,7},{7,6}} | collective-permute-start | bytes 3145736 | tf_op jit(solution)/shard_map/ppermute | solution.py:266
  543.1 95.9 %copy-start.6 = (f32[2,512,512]{2,1,0:T(8,128)S(1)}, f32[2,512,512]{2,1,0:T(8,128)}, u32[]{:S(2)}) copy-start(f32[2,512,512]{2,1,0:T(8,128)} %expert_down.8) | copy-start | bytes 6291460
  545.6 4.9 collective-permute-start.25
  545.9 93.1 %copy-start.4 = (f32[2,512,512]{2,1,0:T(8,128)S(1)}, f32[2,512,512]{2,1,0:T(8,128)}, u32[]{:S(2)}) copy-start(f32[2,512,512]{2,1,0:T(8,128)} %expert_down.14) | copy-start | bytes 6291460
  545.9 93.1 %copy-start.5 = (f32[2,512,512]{2,1,0:T(8,128)S(1)}, f32[2,512,512]{2,1,0:T(8,128)}, u32[]{:S(2)}) copy-start(f32[2,512,512]{2,1,0:T(8,128)} %expert_down.12) | copy-start | bytes 6291460
  546.1 92.9 %copy-start.3 = (bf16[512,2048]{1,0:T(8,128)(2,1)S(1)}, bf16[512,2048]{1,0:T(8,128)(2,1)}, u32[]{:S(2)}) copy-start(bf16[512,2048]{1,0:T(8,128)(2,1)} %get-tuple-element.11) | copy-start | bytes 6291460
  546.2 26.1 %collective-permute-start.40 = (f32[512,512]{1,0:T(8,128)S(1)}, f32[512,512]{1,0:T(8,128)S(1)}, u32[]{:S(2)}, u32[]{:S(2)}) collective-permute-start(f32[512,512]{1,0:T(8,128)S(1)} %fusion.6), channel_id=1, source_target_pairs={{0,2},{2,0},{1,3},{3,1},{4,6},{6,4},{5,7},{7,5}} | collective-permute-start | bytes 3145736 | tf_op jit(solution)/shard_map/ppermute | solution.py:261
  548.3 46.4 %collective-permute-start.37 = (f32[512,512]{1,0:T(8,128)S(1)}, f32[512,512]{1,0:T(8,128)S(1)}, u32[]{:S(2)}, u32[]{:S(2)}) collective-permute-start(f32[512,512]{1,0:T(8,128)S(1)} %fusion.11), channel_id=1, source_target_pairs={{0,2},{2,0},{1,3},{3,1},{4,6},{6,4},{5,7},{7,5}} | collective-permute-start | bytes 3145736 | tf_op jit(solution)/shard_map/ppermute | solution.py:261
  548.5 68.7 %collective-permute-start.34 = (f32[512,512]{1,0:T(8,128)S(1)}, f32[512,512]{1,0:T(8,128)S(1)}, u32[]{:S(2)}, u32[]{:S(2)}) collective-permute-start(f32[512,512]{1,0:T(8,128)S(1)} %fusion.16), channel_id=1, source_target_pairs={{0,2},{2,0},{1,3},{3,1},{4,6},{6,4},{5,7},{7,5}} | collective-permute-start | bytes 3145736 | tf_op jit(solution)/shard_map/ppermute | solution.py:261
  550.3 88.7 %collective-permute-start.31 = (f32[512,512]{1,0:T(8,128)S(1)}, f32[512,512]{1,0:T(8,128)S(1)}, u32[]{:S(2)}, u32[]{:S(2)}) collective-permute-start(f32[512,512]{1,0:T(8,128)S(1)} %fusion.21), channel_id=1, source_target_pairs={{0,2},{2,0},{1,3},{3,1},{4,6},{6,4},{5,7},{7,5}} | collective-permute-start | bytes 3145736 | tf_op jit(solution)/shard_map/ppermute | solution.py:261
  (21 other events, 105.3 us)

commit v2 on v1

--- a/solution.py
+++ b/solution.py
@@ -110,83 +110,248 @@
     )(offs, context, tokens, *pieces)
 
 
-def up_kernel(pos_lane_ref, pos_ref, gate_ref, u0_ref, u1_ref, w1_ref, w3_ref, act_ref, mix_ref, rows_ref, *, cap):
-    expert = pl.program_id(0)
-    seq = u0_ref.shape[0]
+def spread_kernel(pos_ref, out_ref):
+    expert = pl.program_id(1)
+    seq = pos_ref.shape[1]
+    lanes = lax.broadcasted_iota(jnp.int32, (seq, pos_ref.shape[2]), 1)
+    place = jnp.sum(jnp.where(lanes == expert, pos_ref[0], 0), axis=-1, keepdims=True)
+    slots = lax.broadcasted_iota(jnp.int32, (seq, out_ref.shape[2]), 1)
+    out_ref[0] = (place == slots).astype(F32).astype(BF16)
+
+
+def spread(pos, cap):
+    sources, seq, count = pos.shape
+    return pl.pallas_call(
+        spread_kernel,
+        grid=(sources, count),
+        in_specs=[pl.BlockSpec((1, seq, count), lambda s, e: (s, 0, 0))],
+        out_specs=pl.BlockSpec((1, seq, cap), lambda s, e: (s, 0, e)),
+        out_shape=jax.ShapeDtypeStruct((sources, seq, count * cap), BF16),
+        compiler_params=params('arbitrary', 'arbitrary'),
+        name='spread',
+    )(pos)
+
+
+def moe_kernel(pos_ref, u_ref, gate_ref, hid_ref, w1_ref, w3_ref, w2_ref, oh_ref, out_ref,
+               ug, gg, rows, act, gcol, w13, w2t, oht, pst, acc, pair_buf, far_src, far_dst,
+               us, ur, gs, gr, ws, w2s, ohs, ps, pr, xs, xr,
+               *, cap, u_chunks, chunks, groups, wslots):
+    me = lax.axis_index('ep')
+    relations = (me ^ 1, me ^ 2, me ^ 3)
+    seq, model = u_ref.shape
+    count, _, width = w1_ref.shape
+    col = width // wslots
+    block = model // chunks
+    per = count // groups
+    piece = seq // u_chunks
+
+    def remote(src, dst, send, recv, relation):
+        return pltpu.make_async_remote_copy(src_ref=src, dst_ref=dst, send_sem=send, recv_sem=recv,
+                                            device_id={'ep': relations[relation]}, device_id_type=pl.DeviceIdType.MESH)
+
+    def w13_copy(expert, slot, which):
+        ref = (w1_ref, w3_ref)[which]
+        return pltpu.make_async_copy(ref.at[expert, :, pl.ds(slot * col, col)], w13.at[slot, which], ws.at[slot, which])
+
+    def w2_copy(chunk, part, slot):
+        return pltpu.make_async_copy(w2_ref.at[pl.ds(part * per, per), :, pl.ds(pl.multiple_of(chunk * block, block), block)],
+                                     w2t.at[slot], w2s.at[slot])
+
+    def oh_copy(phase, part, slot):
+        return pltpu.make_async_copy(oh_ref.at[pl.ds(2 * phase, 2), :, pl.ds(part * per * cap, per * cap)],
+                                     oht.at[slot], ohs.at[slot])
+
+    for slot in range(wslots):
+        w13_copy(0, slot, 0).start()
+        w13_copy(0, slot, 1).start()
+
+    barrier = pltpu.get_barrier_semaphore()
+    for peer in relations:
+        pl.semaphore_signal(barrier, inc=1, device_id={'ep': peer}, device_id_type=pl.DeviceIdType.MESH)
+    pl.semaphore_wait(barrier, 3)
+
+    gate_sends = [remote(gate_ref.at[pl.ds(pl.multiple_of(relations[r] * count, count), count)], gg.at[r], gs.at[r], gr.at[r], r)
+                  for r in range(3)]
+    pair_send = remote(u_ref, ug.at[0], us.at[0], ur.at[0], 0)
+
+    def far_send(idx):
+        part = pl.ds(idx * piece, piece)
+        return remote(u_ref.at[part], ug.at[1, part], us.at[1 + idx], ur.at[1 + idx], 1)
+
+    def relay_send(idx):
+        part = pl.ds(idx * piece, piece)
+        return remote(ug.at[1, part], ug.at[2, part], us.at[1 + u_chunks + idx], ur.at[1 + u_chunks + idx], 0)
+
+    for send in gate_sends:
+        send.start()
+    for idx in range(u_chunks):
+        far_send(idx).start()
+    pair_send.start()
+
     slots = lax.broadcasted_iota(jnp.int32, (cap, seq), 0)
-    for src, u_ref in enumerate((u0_ref, u1_ref)):
-        pick = (pos_lane_ref[0, src:src + 1, :] == slots).astype(F32).astype(BF16)
-        rows_ref[src * cap:(src + 1) * cap, :] = jnp.dot(pick, u_ref[...], preferred_element_type=F32).astype(BF16)
-    rows = rows_ref[...]
-    first = jnp.dot(rows, w1_ref[0], preferred_element_type=F32)
-    third = jnp.dot(rows, w3_ref[0], preferred_element_type=F32)
-    act_ref[0] = (jax.nn.silu(first) * third).astype(BF16)
-    lanes = lax.broadcasted_iota(jnp.int32, (seq, pos_ref.shape[2]), 1)
-    cap_lanes = lax.broadcasted_iota(jnp.int32, (seq, cap), 1)
-    for src in range(2):
-        place = jnp.sum(jnp.where(lanes == expert, pos_ref[src], 0), axis=-1, keepdims=True)
-        gate = jnp.sum(jnp.where(lanes == expert, gate_ref[src], 0.0), axis=-1, keepdims=True)
-        hit = place == cap_lanes
-        rest = gate
-        for term in range(3):
-            part = rest.astype(BF16).astype(F32)
-            mix_ref[src, :, term * cap:(term + 1) * cap] = jnp.where(hit, part, 0.0).astype(BF16)
-            rest = rest - part
-
-
-def expert_up(pos_lane, pos, gates, u0, u1, w_one, w_three, cap):
-    count, depth, width = w_one.shape
-    seq = u0.shape[0]
-    whole2 = pl.BlockSpec((seq, depth), lambda e: (0, 0))
-    whole3 = pl.BlockSpec((2, seq, count), lambda e: (0, 0, 0))
-    w_spec = pl.BlockSpec((1, depth, width), lambda e: (e, 0, 0))
+    lanes = lax.broadcasted_iota(jnp.int32, (2 * cap, 128), 1)
+
+    def up_step(phase, expert):
+        place = pos_ref[expert]
+        if phase == 0:
+            sources = ((u_ref[...], gate_ref[pl.ds(me * count + expert, 1), :]), (ug[0], gg[0, pl.ds(expert, 1), :]))
+        else:
+            sources = ((ug[1], gg[1, pl.ds(expert, 1), :]), (ug[2], gg[2, pl.ds(expert, 1), :]))
+        for src, (u_val, gate_row) in enumerate(sources):
+            hit = place[2 * phase + src:2 * phase + src + 1, :] == slots
+            rows[src * cap:(src + 1) * cap, :] = jnp.dot(hit.astype(F32).astype(BF16), u_val,
+                                                         preferred_element_type=F32).astype(BF16)
+            column = jnp.sum(jnp.where(hit, gate_row, 0.0), axis=-1, keepdims=True)
+            part = slice(src * cap, (src + 1) * cap)
+            gcol[phase, part, :] = jnp.where(lanes[part] == expert, column, gcol[phase, part, :])
+        for slot in range(wslots):
+            w13_copy(0, slot, 0).wait()
+            w13_copy(0, slot, 1).wait()
+            first = jnp.dot(rows[...], w13[slot, 0], preferred_element_type=F32)
+            third = jnp.dot(rows[...], w13[slot, 1], preferred_element_type=F32)
+            act[phase * count + expert, :, slot * col:(slot + 1) * col] = (jax.nn.silu(first) * third).astype(BF16)
+
+            def refill(slot=slot):
+                following = lax.rem(expert + 1, count)
+                w13_copy(following, slot, 0).start()
+                w13_copy(following, slot, 1).start()
+
+            if phase == 0:
+                refill()
+            else:
+                pl.when(expert < count - 1)(refill)
+
+    gcol[...] = jnp.zeros_like(gcol)
+    gate_sends[0].wait_recv()
+    pair_send.wait_recv()
+    step = count // u_chunks
+    for idx in range(u_chunks):
+        def near(expert, carry):
+            up_step(0, expert)
+            return carry
+        lax.fori_loop(idx * step, (idx + 1) * step, near, 0)
+        far_send(idx).wait_recv()
+        relay_send(idx).start()
+    for idx in range(3):
+        w2_copy(0, idx, idx).start()
+        oh_copy(1, idx, idx).start()
+    gate_sends[1].wait_recv()
+    gate_sends[2].wait_recv()
+    for idx in range(u_chunks):
+        relay_send(idx).wait_recv()
+
+    def away(expert, carry):
+        up_step(1, expert)
+        return carry
+    lax.fori_loop(0, count, away, 0)
+
+    def down_chunk(phase, chunk):
+        order = (1 - phase) * chunks + chunk
+        for part in range(groups):
+            slot = lax.rem(order * groups + part, 3)
+            w2_copy(0, 0, slot).wait()
+            oh_copy(0, 0, slot).wait()
+            for idx in range(per):
+                expert = part * per + idx
+                done = jnp.dot(act[phase * count + expert], w2t[slot, idx], preferred_element_type=F32).astype(BF16)
+                rest = done.astype(F32) * gcol[phase, :, expert:expert + 1]
+                for term in range(3):
+                    head = rest.astype(BF16)
+                    at = (term * per + idx) * cap
+                    pst[0, at:at + cap, :] = head[:cap]
+                    pst[1, at:at + cap, :] = head[cap:]
+                    rest = rest - head.astype(F32)
+            depth = per * cap
+            for src in range(2):
+                mixed = jnp.dot(oht[slot, src], pst[src, 0:depth, :], preferred_element_type=F32)
+                for term in range(1, 3):
+                    mixed += jnp.dot(oht[slot, src], pst[src, term * depth:(term + 1) * depth, :], preferred_element_type=F32)
+                if part == 0:
+                    acc[lax.rem(chunk, 2), src] = mixed
+                else:
+                    acc[lax.rem(chunk, 2), src] += mixed
+
+            def refill(part=part, slot=slot):
+                ahead = order * groups + part + 3
+                ahead_chunk = lax.rem(ahead // groups, chunks)
+                ahead_part = lax.rem(ahead, groups)
+                ahead_phase = 1 - ahead // (groups * chunks)
+                w2_copy(ahead_chunk, ahead_part, slot).start()
+                oh_copy(ahead_phase, ahead_part, slot).start()
+
+            if phase == 1:
+                refill()
+            else:
+                pl.when(order * groups + part + 3 < 2 * groups * chunks)(refill)
+
+    def pair_sum(phase, chunk):
+        slot = lax.rem((1 - phase) * chunks + chunk, 4)
+        return remote(acc.at[lax.rem(chunk, 2), 1], pair_buf.at[slot], ps.at[slot], pr.at[slot], 0)
+
+    def far_sum(chunk):
+        return remote(far_src.at[chunk], far_dst.at[chunk], xs.at[chunk], xr.at[chunk], 1)
+
+    def settle(phase, chunk):
+        pair_sum(phase, chunk).wait_recv()
+        pair_sum(phase, chunk).wait_send()
+        slot = lax.rem((1 - phase) * chunks + chunk, 4)
+        total = acc[lax.rem(chunk, 2), 0] + pair_buf[slot]
+        if phase == 1:
+            far_src[chunk] = total
+            far_sum(chunk).start()
+        else:
+            far_sum(chunk).wait_recv()
+            cols = pl.ds(pl.multiple_of(chunk * block, block), block)
+            out_ref[:, cols] = (hid_ref[:, cols].astype(F32) + total + far_dst[chunk]).astype(BF16)
+
+    for phase in (1, 0):
+        def down(chunk, carry, phase=phase):
+            down_chunk(phase, chunk)
+
+            @pl.when(chunk > 0)
+            def _():
+                settle(phase, chunk - 1)
+
+            pair_sum(phase, chunk).start()
+            return carry
+        lax.fori_loop(0, chunks, down, 0)
+        settle(phase, chunks - 1)
+
+    for send in gate_sends:
+        send.wait_send()
+    pair_send.wait_send()
+    for idx in range(u_chunks):
+        far_send(idx).wait_send()
+        relay_send(idx).wait_send()
+    for idx in range(chunks):
+        far_sum(idx).wait_send()
+
+
+def moe(pos_lane, u_own, gates_lane, hidden, w_one, w_three, w_two, onehot, cap):
+    seq, model = u_own.shape
+    count, _, width = w_one.shape
+    u_chunks, chunks, groups, wslots = 4, 8, 4, 4
+    block, per = model // chunks, count // groups
+    vmem = pl.BlockSpec(memory_space=pltpu.VMEM)
+    hbm = pl.BlockSpec(memory_space=pl.ANY)
+    dma = pltpu.SemaphoreType.DMA
     return pl.pallas_call(
-        functools.partial(up_kernel, cap=cap),
-        grid=(count,),
-        in_specs=[pl.BlockSpec((1, 2, seq), lambda e: (e, 0, 0)), whole3, whole3, whole2, whole2, w_spec, w_spec],
-        out_specs=[pl.BlockSpec((1, 2 * cap, width), lambda e: (e, 0, 0)),
-                   pl.BlockSpec((2, seq, 3 * cap), lambda e: (0, 0, e))],
-        out_shape=[jax.ShapeDtypeStruct((count, 2 * cap, width), BF16),
-                   jax.ShapeDtypeStruct((2, seq, count * 3 * cap), BF16)],
-        scratch_shapes=[pltpu.VMEM((2 * cap, depth), BF16)],
-        compiler_params=params('arbitrary'),
-        cost_estimate=pl.CostEstimate(flops=8 * cap * depth * width * count + 4 * cap * seq * depth * count,
-                                      bytes_accessed=4 * count * depth * width, transcendentals=0),
-        name='expert_up',
-    )(pos_lane, pos, gates, u0, u1, w_one, w_three)
-
-
-def down_kernel(act_ref, w2_ref, mix_ref, out_ref, *, cap, per):
-    @pl.when(pl.program_id(0) == 0)
-    def _():
-        out_ref[...] = jnp.zeros_like(out_ref)
-
-    stack = [[], []]
-    for idx in range(per):
-        done = jnp.dot(act_ref[idx], w2_ref[idx], preferred_element_type=F32).astype(BF16)
-        for src in range(2):
-            stack[src] += [done[src * cap:(src + 1) * cap]] * 3
-    for src in range(2):
-        out_ref[src] += jnp.dot(mix_ref[src], jnp.concatenate(stack[src], axis=0), preferred_element_type=F32)
-
-
-def expert_down(act, w_two, mix, cap, part, parts, per=2):
-    count, width, model = w_two.shape
-    seq = mix.shape[1]
-    block = model // parts
-    return pl.pallas_call(
-        functools.partial(down_kernel, cap=cap, per=per),
-        grid=(count // per,),
-        in_specs=[pl.BlockSpec((per, 2 * cap, width), lambda e: (e, 0, 0)),
-                  pl.BlockSpec((per, width, block), lambda e: (e, 0, part)),
-                  pl.BlockSpec((2, seq, 3 * cap * per), lambda e: (0, 0, e))],
-        out_specs=pl.BlockSpec((2, seq, block), lambda e: (0, 0, 0)),
-        out_shape=jax.ShapeDtypeStruct((2, seq, block), F32),
-        compiler_params=params('arbitrary'),
-        cost_estimate=pl.CostEstimate(flops=(4 * cap * width * block + 12 * seq * cap * block) * count,
-                                      bytes_accessed=2 * count * width * block, transcendentals=0),
-        name='expert_down',
-    )(act, w_two, mix)
+        functools.partial(moe_kernel, cap=cap, u_chunks=u_chunks, chunks=chunks, groups=groups, wslots=wslots),
+        in_specs=[vmem, vmem, vmem, vmem, hbm, hbm, hbm, hbm],
+        out_specs=vmem,
+        out_shape=jax.ShapeDtypeStruct((seq, model), BF16),
+        scratch_shapes=[
+            pltpu.VMEM((3, seq, model), BF16), pltpu.VMEM((3, count, seq), F32), pltpu.VMEM((2 * cap, model), BF16),
+            pltpu.VMEM((2 * count, 2 * cap, width), BF16), pltpu.VMEM((2, 2 * cap, 128), F32),
+            pltpu.VMEM((wslots, 2, model, width // wslots), BF16), pltpu.VMEM((3, per, width, block), BF16),
+            pltpu.VMEM((3, 2, seq, per * cap), BF16), pltpu.VMEM((2, 3 * per * cap, block), BF16),
+            pltpu.VMEM((2, 2, seq, block), F32), pltpu.VMEM((4, seq, block), F32),
+            pltpu.VMEM((chunks, seq, block), F32), pltpu.VMEM((chunks, seq, block), F32),
+            dma((1 + 2 * u_chunks,)), dma((1 + 2 * u_chunks,)), dma((3,)), dma((3,)), dma((wslots, 2)), dma((3,)), dma((3,)),
+            dma((4,)), dma((4,)), dma((chunks,)), dma((chunks,))],
+        compiler_params=pltpu.CompilerParams(collective_id=1, has_side_effects=True, vmem_limit_bytes=67043328),
+        name='moe',
+    )(pos_lane, u_own, gates_lane, hidden, w_one, w_three, w_two, onehot)
 
 
 def solution(mesh):
@@ -239,32 +404,9 @@
         context = attend(query, keys, values, head_dim)
         hidden, u_own = out_project(offs, context, x_rows, o_parts)
 
-        u_far = across(u_own)
-        u_pair = pair(u_own)
-        u_far_pair = pair(u_far)
-
         logits = jnp.dot(rms_norm(hidden), w_router, precision=lax.Precision.HIGHEST, preferred_element_type=F32)
         chosen = jnp.any(ids[:, :, None] == jnp.arange(experts, dtype=jnp.int32), axis=1)
         gates = jax.nn.softmax(jnp.where(chosen, logits, -jnp.inf), axis=-1)
-        gates_far = across(gates)
-        pick = functools.partial(lax.dynamic_slice_in_dim, start_index=me * own_experts, slice_size=own_experts, axis=1)
-        gates_near = jnp.stack([pick(gates), pick(pair(gates))])
-        gates_away = jnp.stack([pick(gates_far), pick(pair(gates_far))])
-
-        act_near, mix_near = expert_up(pos_lane[:, 0:2], pos[0:2], gates_near, u_own, u_pair, w_one, w_three, cap)
-        act_away, mix_away = expert_up(pos_lane[:, 2:4], pos[2:4], gates_away, u_far, u_far_pair, w_one, w_three, cap)
-
-        parts = 4
-        back = []
-        for part in range(parts):
-            sums = expert_down(act_away, w_two, mix_away, cap, part, parts)
-            back.append(across(sums[0] + pair(sums[1])))
-        outs = []
-        for part in range(parts):
-            sums = expert_down(act_near, w_two, mix_near, cap, part, parts)
-            block = model // parts
-            near = hidden[:, part * block:(part + 1) * block].astype(F32) + (sums[0] + pair(sums[1]))
-            outs.append((near + back[part]).astype(BF16))
-        return jnp.concatenate(outs, axis=1)[None]
+        return moe(pos_lane, u_own, gates.T, hidden, w_one, w_three, w_two, spread(pos, cap), cap)[None]
 
     return jax.shard_map(local_layer, mesh=mesh, in_specs=(tok_spec, row_spec, row_spec, row_spec, row_spec, P(), row_spec, row_spec, row_spec, tok_spec), out_specs=tok_spec, check_vma=False)

time: 644 us -> 494 us (0.77)
  waiting for transfers between devices: 232 us -> 114 us
  local copies, waits for them, and re-layouts: 30.9 us -> 15.8 us
  starting transfers between devices: 25 us -> 14.6 us
  Pallas kernels: 335 us -> 328 us
    ppermute x18 -> x0, waiting for transfers between devices: 90.3 us -> none  [the longest x8 88.5 us: local_layer(): back.append(across(sums[0] + pair(sums[1])))]
    ppermute x4, waiting for transfers between devices: 56.4 us -> 31 us  [gather(): far_other = swap(far)]
    squeeze x8 -> x0, local copies, waits for them, and re-layouts: 10.6 us -> none  [the longest x4 6.93 us: local_layer(): sums[1]]
    ppermute x18 -> x0, starting transfers between devices: 8.43 us -> none  [the longest x8 5 us: local_layer(): back.append(across(sums[0] + pair(sums[1])))]
    pallas_call x10 -> x2, Pallas kernels: 275 us -> 268 us  [the longest x1 238 us: moe(): pl.pallas_call(functools.partial(moe_kernel, cap=cap, u_chunks=u_chunks,...]
  transfers between devices with their start and end apart: 41 -> 23, of which waited for: 14 -> 6; matrix products, arithmetic and copies ran while one was open for 6% -> 3% of each run, Pallas kernels for 50% -> 16%
where the time goes in v2:
time: 494 us; the launch traced here: 489 us
  Pallas kernels  328 us (66%)
  waiting for transfers between devices  114 us (23%)
  local copies, waits for them, and re-layouts  15.8 us (3%)
  starting transfers between devices  14.6 us (3%)
  other arithmetic  11.3 us (2%)
    pallas_call x1, Pallas kernels, moe(): pl.pallas_call(functools.partial(moe_kernel, cap=cap, u_chunks=u_chunks,...  238 us
    ppermute x1, waiting for transfers between devices, local_layer(): ids_far = across(ids)  42.2 us
    ppermute x4, waiting for transfers between devices, gather(): far = across(mine)  39.8 us
    ppermute x4, waiting for transfers between devices, gather(): far_other = swap(far)  31 us
    pallas_call x1, Pallas kernels, spread(): pl.pallas_call(spread_kernel, grid=(sources, count), in_specs=[pl.BlockSp...  30.8 us
    pallas_call x3, Pallas kernels, project(): pl.pallas_call(proj_kernel, grid=(cols // block,), in_specs=[pl.BlockSpec...  27 us
    pallas_call x1, Pallas kernels, attend(): pl.pallas_call(functools.partial(attn_kernel, rows=128, scale=head_dim **...  22.2 us
    unnamed x39, local copies, waits for them, and re-layouts  11.1 us
  transfers between devices with their start and end apart: 23, of which 6 were waited for; matrix products, arithmetic and copies ran while one was open for 3% of the time, Pallas kernels for 16%

profile of v2, /device:TPU:0, one launch (start us, length us, event | category | flops | bytes accessed | tf_op | source)
XLA Modules:
  0.0 488.8 jit_solution(14527287507528545290)
XLA Ops:
  0.0 1.6 constant_dynamic-slice_fusion.2
  1.6 0.3 copy.46
  1.9 3.4 collective-permute-start.9
  5.2 0.2 constant_dynamic-slice_fusion.1
  5.4 0.3 copy.45
  5.8 0.5 copy.43
  6.5 2.0 collective-permute-start.1
  8.6 0.2 constant_dynamic-slice_fusion.3
  8.7 0.3 copy.47
  9.0 42.2 %collective-permute-done.1 = s32[512,8]{0,1:T(8,128)S(1)} collective-permute-done((s32[512,8]{0,1:T(8,128)S(1)}, s32[512,8]{0,1:T(8,128)S(1)}, u32[]{:S(2)}, u32[]{:S(2)}) %collective-permute-start.1) | collective-permute-done | bytes 16416 | tf_op jit(solution)/shard_map/ppermute | solution.py:392
  51.2 1.7 collective-permute-start.4
  53.0 1.1 collective-permute-done.2
  54.1 0.3 collective-permute-start.19
  54.4 1.8 collective-permute-start.10
  56.2 1.9 copy.42
  58.2 19.1 %collective-permute-done.4.refs_2_ = bf16[256,2048]{1,0:T(8,128)(2,1)} collective-permute-done((bf16[256,2048]{1,0:T(8,128)(2,1)S(1)}, bf16[256,2048]{1,0:T(8,128)(2,1)}, u32[]{:S(2)}, u32[]{:S(2)}) %collective-permute-start.4) | collective-permute-done | bytes 1048608 | tf_op jit(solution)/shard_map/ppermute | solution.py:381
  77.2 20.8 %collective-permute-done.19.refs_2_ = bf16[256,2048]{1,0:T(8,128)(2,1)S(1)} collective-permute-done((bf16[256,2048]{1,0:T(8,128)(2,1)S(1)}, bf16[256,2048]{1,0:T(8,128)(2,1)S(1)}, u32[]{:S(2)}, u32[]{:S(2)}) %collective-permute-start.19) | collective-permute-done | bytes 1048608 | tf_op jit(solution)/shard_map/ppermute | solution.py:381
  98.0 1.5 collective-permute-start.15
  99.5 0.5 fusion
  100.0 0.6 collective-permute-start.5
  100.6 1.3 copy-done.9
  101.9 0.3 collective-permute-start.6
  102.2 1.7 fusion.1.left_ref
  103.9 1.9 copy.44
  105.8 18.2 %collective-permute-done.15.refs_3_ = bf16[256,2048]{1,0:T(8,128)(2,1)} collective-permute-done((bf16[256,2048]{1,0:T(8,128)(2,1)S(1)}, bf16[256,2048]{1,0:T(8,128)(2,1)}, u32[]{:S(2)}, u32[]{:S(2)}) %collective-permute-start.15) | collective-permute-done | bytes 1048608 | tf_op jit(solution)/shard_map/ppermute | solution.py:382
  124.2 0.5 collective-permute-start.3
  124.7 0.7 stack.43.offs_ref
  125.4 0.2 compare_reduce_fusion
  125.7 4.8 reduce-window.6
  130.6 0.4 slice_reduce_fusion
  131.2 12.8 %collective-permute-done.5.refs_3_ = bf16[256,2048]{1,0:T(8,128)(2,1)} collective-permute-done((bf16[256,2048]{1,0:T(8,128)(2,1)}, bf16[256,2048]{1,0:T(8,128)(2,1)}, u32[]{:S(2)}, u32[]{:S(2)}) %collective-permute-start.5) | collective-permute-done | bytes 1048608 | tf_op jit(solution)/shard_map/ppermute | solution.py:382
  143.9 1.2 collective-permute-start.20
  145.4 0.5 collective-permute-start.7
  146.0 1.3 copy.26.pos_ref
  147.4 30.8 %spread.1.oh_ref = bf16[4,512,2048]{2,1,0:T(8,128)(2,1)} custom-call(s32[4,512,16]{2,1,0:T(8,128)} %copy.26.pos_ref), custom_call_target="tpu_custom_call" | custom-call | tf_op jit(solution)/shard_map/spread/pallas_call | solution.py:124
  178.2 0.7 fusion.8.pos_ref
  178.9 9.0 %project.4.k_ref = bf16[512,2048]{1,0:T(8,128)(2,1)} custom-call(s32[6]{0:T(128)} %stack.43.offs_ref, bf16[512,2048]{1,0:T(8,128)(2,1)} %fusion.1.left_ref, bf16[512,2048]{1,0:T(8,128)(2,1)} %bitcast.64, bf16[512,2048]{1,0:T(8,128)(2,1)} %copy-done.9, bf16[256,2048]{1,0:T(8,128)(2,1)} %copy-done.13, bf16[256,2048]{1,0:T(8,128)(2,1)} %copy-done.14, ...), custom_call_target="tpu_custom_call" | custom-call | flops 4294967296 | bytes 8388608 | tf_op jit(solution)/shard_map/project/pallas_call | solution.py:45
  187.9 0.5 collective-permute-start.22
  188.4 9.0 %project.5.v_ref = bf16[512,2048]{1,0:T(8,128)(2,1)} custom-call(s32[6]{0:T(128)} %stack.43.offs_ref, bf16[512,2048]{1,0:T(8,128)(2,1)} %fusion.1.left_ref, bf16[512,2048]{1,0:T(8,128)(2,1)} %bitcast.49.refs_0_, bf16[512,2048]{1,0:T(8,128)(2,1)} %collective-permute-done.13.refs_1_, bf16[256,2048]{1,0:T(8,128)(2,1)} %copy-done.11, ...), custom_call_target="tpu_custom_call" | custom-call | flops 4294967296 | bytes 8388608 | tf_op jit(solution)/shard_map/project/pallas_call | solution.py:45
  197.5 9.0 %project.3.q_ref = bf16[512,2048]{1,0:T(8,128)(2,1)} custom-call(s32[6]{0:T(128)} %stack.43.offs_ref, bf16[512,2048]{1,0:T(8,128)(2,1)} %fusion.1.left_ref, bf16[512,2048]{1,0:T(8,128)(2,1)} %bitcast.66, bf16[512,2048]{1,0:T(8,128)(2,1)} %collective-permute-done.3.refs_1_, bf16[256,2048]{1,0:T(8,128)(2,1)} %collective-permute-done.4.refs_2_, ...), custom_call_target="tpu_custom_call" | custom-call | flops 4294967296 | bytes 8388608 | tf_op jit(solution)/shard_map/project/pallas_call | solution.py:45
  206.4 22.2 %attend.1.left_ref = bf16[512,2048]{1,0:T(8,128)(2,1)} custom-call(bf16[512,2048]{1,0:T(8,128)(2,1)} %project.3.q_ref, bf16[512,2048]{1,0:T(8,128)(2,1)} %project.4.k_ref, bf16[512,2048]{1,0:T(8,128)(2,1)} %project.5.v_ref), custom_call_target="tpu_custom_call" | custom-call | flops 4294967296 | bytes 8388608 | tf_op jit(solution)/shard_map/attend/pallas_call | solution.py:78
  228.7 1.3 copy-done.10
  230.0 10.4 %out_project.1 = (bf16[512,2048]{1,0:T(8,128)(2,1)}, bf16[512,2048]{1,0:T(8,128)(2,1)}) custom-call(s32[6]{0:T(128)} %stack.43.offs_ref, bf16[512,2048]{1,0:T(8,128)(2,1)} %attend.1.left_ref, bf16[512,2048]{1,0:T(8,128)(2,1)} %bitcast.56, bf16[512,2048]{1,0:T(8,128)(2,1)} %refs_0_.1, bf16[512,2048]{1,0:T(8,128)(2,1)} %copy-done.10, ...), custom_call_target="tpu_custom_call" | custom-call | flops 4294967296 | bytes 8388608 | tf_op jit(solution)/shard_map/out_project/pallas_call | solution.py:100
  240.4 2.2 fusion.2
  242.7 4.5 fusion.10
  247.2 0.7 divide_bitcast_fusion.gate_ref
  247.9 237.6 %moe.1 = bf16[512,2048]{1,0:T(8,128)(2,1)} custom-call(s32[16,4,512]{2,1,0:T(4,128)} %fusion.8.pos_ref, bf16[512,2048]{1,0:T(8,128)(2,1)} %get-tuple-element.7.u_ref, f32[64,512]{1,0:T(8,128)} %divide_bitcast_fusion.gate_ref, bf16[512,2048]{1,0:T(8,128)(2,1)} %get-tuple-element.8.hid_ref, bf16[16,2048,1024]{2,1,0:T(8,128)(2,1)} %w1_ref.1, ...), custom_call_target="tpu_custom_call" | custom-call | tf_op jit(solution)/shard_map/moe/pallas_call | solution.py:338
  485.4 3.2 copy.49
  (74 shorter events, 1.3 us)
Async XLA Ops:
  0.0 5.2 %copy-start.3 = (bf16[512,16,128]{2,1,0:T(8,128)(2,1)S(1)}, bf16[512,16,128]{2,1,0:T(8,128)(2,1)}, u32[]{:S(2)}) copy-start(bf16[512,16,128]{2,1,0:T(8,128)(2,1)} %param.13) | copy-start | bytes 6291460
  1.8 3.9 copy-start.2
  1.9 52.6 %collective-permute-start.9 = (bf16[256,2048]{1,0:T(8,128)(2,1)S(1)}, bf16[256,2048]{1,0:T(8,128)(2,1)S(1)}, u32[]{:S(2)}, u32[]{:S(2)}) collective-permute-start(bf16[256,2048]{1,0:T(8,128)(2,1)S(1)} %bitcast.68), channel_id=1, source_target_pairs={{0,2},{2,0},{1,3},{3,1},{4,6},{6,4},{5,7},{7,5}} | collective-permute-start | bytes 3145736 | tf_op jit(solution)/shard_map/ppermute | solution.py:381
  5.7 50.5 %collective-permute-start.14 = (bf16[256,2048]{1,0:T(8,128)(2,1)S(1)}, bf16[256,2048]{1,0:T(8,128)(2,1)S(1)}, u32[]{:S(2)}, u32[]{:S(2)}) collective-permute-start(bf16[256,2048]{1,0:T(8,128)(2,1)S(1)} %bitcast.67), channel_id=1, source_target_pairs={{0,2},{2,0},{1,3},{3,1},{4,6},{6,4},{5,7},{7,5}} | collective-permute-start | bytes 3145736 | tf_op jit(solution)/shard_map/ppermute | solution.py:381
  5.7 0.7 copy-start.8
  5.7 2.8 copy-start.4
  6.3 2.7 copy-start.5
  6.3 94.3 %collective-permute-start.8 = (bf16[512,2048]{1,0:T(8,128)(2,1)S(1)}, bf16[512,2048]{1,0:T(8,128)(2,1)S(1)}, u32[]{:S(2)}, u32[]{:S(2)}) collective-permute-start(bf16[512,2048]{1,0:T(8,128)(2,1)S(1)} %bitcast.63), channel_id=1, source_target_pairs={{0,1},{1,0},{2,3},{3,2},{4,5},{5,4},{6,7},{7,6}} | collective-permute-start | bytes 6291464 | tf_op jit(solution)/shard_map/ppermute | solution.py:383
  6.5 46.5 %copy-start.6 = (bf16[512,2048]{1,0:T(8,128)(2,1)S(1)}, bf16[512,2048]{1,0:T(8,128)(2,1)}, u32[]{:S(2)}) copy-start(bf16[512,2048]{1,0:T(8,128)(2,1)} %refs_0_.1) | copy-start | bytes 6291460
  6.5 44.7 %collective-permute-start.1 = (s32[512,8]{0,1:T(8,128)S(1)}, s32[512,8]{0,1:T(8,128)S(1)}, u32[]{:S(2)}, u32[]{:S(2)}) collective-permute-start(s32[512,8]{0,1:T(8,128)S(1)} %bitcast.70), channel_id=1, source_target_pairs={{0,2},{2,0},{1,3},{3,1},{4,6},{6,4},{5,7},{7,5}} | collective-permute-start | bytes 49160 | tf_op jit(solution)/shard_map/ppermute | solution.py:392
  8.5 44.5 %collective-permute-start = (s32[512,8]{0,1:T(8,128)S(1)}, s32[512,8]{0,1:T(8,128)S(1)}, u32[]{:S(2)}, u32[]{:S(2)}) collective-permute-start(s32[512,8]{0,1:T(8,128)S(1)} %bitcast.71), channel_id=1, source_target_pairs={{0,1},{1,0},{2,3},{3,2},{4,5},{5,4},{6,7},{7,6}} | collective-permute-start | bytes 49160 | tf_op jit(solution)/shard_map/ppermute | solution.py:391
  51.2 26.0 %collective-permute-start.4 = (bf16[256,2048]{1,0:T(8,128)(2,1)S(1)}, bf16[256,2048]{1,0:T(8,128)(2,1)}, u32[]{:S(2)}, u32[]{:S(2)}) collective-permute-start(bf16[256,2048]{1,0:T(8,128)(2,1)S(1)} %bitcast.69), channel_id=1, source_target_pairs={{0,2},{2,0},{1,3},{3,1},{4,6},{6,4},{5,7},{7,5}} | collective-permute-start | bytes 3145736 | tf_op jit(solution)/shard_map/ppermute | solution.py:381
  52.9 1.2 collective-permute-start.2
  54.1 43.9 %collective-permute-start.19 = (bf16[256,2048]{1,0:T(8,128)(2,1)S(1)}, bf16[256,2048]{1,0:T(8,128)(2,1)S(1)}, u32[]{:S(2)}, u32[]{:S(2)}) collective-permute-start(bf16[256,2048]{1,0:T(8,128)(2,1)S(1)} %constant_dynamic-slice_fusion), channel_id=1, source_target_pairs={{0,2},{2,0},{1,3},{3,1},{4,6},{6,4},{5,7},{7,5}} | collective-permute-start | bytes 3145736 | tf_op jit(solution)/shard_map/ppermute | solution.py:381
  54.4 3.7 copy-start.13
  54.4 45.1 %collective-permute-start.10 = (bf16[256,2048]{1,0:T(8,128)(2,1)S(1)}, bf16[256,2048]{1,0:T(8,128)(2,1)S(1)}, u32[]{:S(2)}, u32[]{:S(2)}) collective-permute-start(bf16[256,2048]{1,0:T(8,128)(2,1)S(1)} %collective-permute-done.9.refs_2_), channel_id=1, source_target_pairs={{0,4},{4,0},{1,5},{5,1},{2,6},{6,2},{3,7},{7,3}} | collective-permute-start | bytes 3145736 | tf_op jit(solution)/shard_map/ppermute | solution.py:382
  56.2 43.3 %copy-start.11 = (bf16[256,2048]{1,0:T(8,128)(2,1)}, bf16[256,2048]{1,0:T(8,128)(2,1)S(1)}, u32[]{:S(2)}) copy-start(bf16[256,2048]{1,0:T(8,128)(2,1)S(1)} %collective-permute-done.14.refs_2_) | copy-start | bytes 3145732
  56.2 43.8 %collective-permute-start.11 = (bf16[256,2048]{1,0:T(8,128)(2,1)S(1)}, bf16[256,2048]{1,0:T(8,128)(2,1)S(1)}, u32[]{:S(2)}, u32[]{:S(2)}) collective-permute-start(bf16[256,2048]{1,0:T(8,128)(2,1)S(1)} %collective-permute-done.9.refs_2_), channel_id=1, source_target_pairs={{0,1},{1,0},{2,3},{3,2},{4,5},{5,4},{6,7},{7,6}} | collective-permute-start | bytes 3145736 | tf_op jit(solution)/shard_map/ppermute | solution.py:383
  56.2 43.3 %copy-start.1 = (bf16[1,512,2048]{2,1,0:T(8,128)(2,1)S(1)}, bf16[1,512,2048]{2,1,0:T(8,128)(2,1)}, u32[]{:S(2)}) copy-start(bf16[1,512,2048]{2,1,0:T(8,128)(2,1)} %param.10) | copy-start | bytes 6291460
  77.2 53.9 %collective-permute-start.13 = (bf16[512,2048]{1,0:T(8,128)(2,1)}, bf16[512,2048]{1,0:T(8,128)(2,1)}, u32[]{:S(2)}, u32[]{:S(2)}) collective-permute-start(bf16[512,2048]{1,0:T(8,128)(2,1)} %bitcast.49.refs_0_), channel_id=1, source_target_pairs={{0,1},{1,0},{2,3},{3,2},{4,5},{5,4},{6,7},{7,6}} | collective-permute-start | bytes 6291464 | tf_op jit(solution)/shard_map/ppermute | solution.py:383
  98.0 4.2 copy-start.12
  98.0 26.0 %collective-permute-start.15 = (bf16[256,2048]{1,0:T(8,128)(2,1)S(1)}, bf16[256,2048]{1,0:T(8,128)(2,1)}, u32[]{:S(2)}, u32[]{:S(2)}) collective-permute-start(bf16[256,2048]{1,0:T(8,128)(2,1)S(1)} %collective-permute-done.14.refs_2_), channel_id=1, source_target_pairs={{0,4},{4,0},{1,5},{5,1},{2,6},{6,2},{3,7},{7,3}} | collective-permute-start | bytes 3145736 | tf_op jit(solution)/shard_map/ppermute | solution.py:382
  99.5 2.7 copy-start.14
  99.5 24.7 %collective-permute-start.16 = (bf16[256,2048]{1,0:T(8,128)(2,1)S(1)}, bf16[256,2048]{1,0:T(8,128)(2,1)}, u32[]{:S(2)}, u32[]{:S(2)}) collective-permute-start(bf16[256,2048]{1,0:T(8,128)(2,1)S(1)} %collective-permute-done.14.refs_2_), channel_id=1, source_target_pairs={{0,1},{1,0},{2,3},{3,2},{4,5},{5,4},{6,7},{7,6}} | collective-permute-start | bytes 3145736 | tf_op jit(solution)/shard_map/ppermute | solution.py:383
  100.0 2.2 copy-start.15
  100.0 43.9 %collective-permute-start.5 = (bf16[256,2048]{1,0:T(8,128)(2,1)}, bf16[256,2048]{1,0:T(8,128)(2,1)}, u32[]{:S(2)}, u32[]{:S(2)}) collective-permute-start(bf16[256,2048]{1,0:T(8,128)(2,1)} %collective-permute-done.4.refs_2_), channel_id=1, source_target_pairs={{0,4},{4,0},{1,5},{5,1},{2,6},{6,2},{3,7},{7,3}} | collective-permute-start | bytes 3145736 | tf_op jit(solution)/shard_map/ppermute | solution.py:382
  100.6 1.3 copy-start.9
  101.9 43.2 %collective-permute-start.6 = (bf16[256,2048]{1,0:T(8,128)(2,1)}, bf16[256,2048]{1,0:T(8,128)(2,1)}, u32[]{:S(2)}, u32[]{:S(2)}) collective-permute-start(bf16[256,2048]{1,0:T(8,128)(2,1)} %collective-permute-done.4.refs_2_), channel_id=1, source_target_pairs={{0,1},{1,0},{2,3},{3,2},{4,5},{5,4},{6,7},{7,6}} | collective-permute-start | bytes 3145736 | tf_op jit(solution)/shard_map/ppermute | solution.py:383
  124.0 21.4 %collective-permute-start.12 = (bf16[256,2048]{1,0:T(8,128)(2,1)}, bf16[256,2048]{1,0:T(8,128)(2,1)}, u32[]{:S(2)}, u32[]{:S(2)}) collective-permute-start(bf16[256,2048]{1,0:T(8,128)(2,1)} %copy-done.14), channel_id=1, source_target_pairs={{0,1},{1,0},{2,3},{3,2},{4,5},{5,4},{6,7},{7,6}} | collective-permute-start | bytes 3145736 | tf_op jit(solution)/shard_map/ppermute | solution.py:383
  124.2 73.3 %collective-permute-start.3 = (bf16[512,2048]{1,0:T(8,128)(2,1)}, bf16[512,2048]{1,0:T(8,128)(2,1)}, u32[]{:S(2)}, u32[]{:S(2)}) collective-permute-start(bf16[512,2048]{1,0:T(8,128)(2,1)} %bitcast.65), channel_id=1, source_target_pairs={{0,1},{1,0},{2,3},{3,2},{4,5},{5,4},{6,7},{7,6}} | collective-permute-start | bytes 6291464 | tf_op jit(solution)/shard_map/ppermute | solution.py:383
  131.1 97.6 %collective-permute-start.18 = (bf16[512,2048]{1,0:T(8,128)(2,1)}, bf16[512,2048]{1,0:T(8,128)(2,1)S(1)}, u32[]{:S(2)}, u32[]{:S(2)}) collective-permute-start(bf16[512,2048]{1,0:T(8,128)(2,1)} %refs_0_.1), channel_id=1, source_target_pairs={{0,1},{1,0},{2,3},{3,2},{4,5},{5,4},{6,7},{7,6}} | collective-permute-start | bytes 6291464 | tf_op jit(solution)/shard_map/ppermute | solution.py:383
  143.9 43.9 %collective-permute-start.20 = (bf16[256,2048]{1,0:T(8,128)(2,1)}, bf16[256,2048]{1,0:T(8,128)(2,1)}, u32[]{:S(2)}, u32[]{:S(2)}) collective-permute-start(bf16[256,2048]{1,0:T(8,128)(2,1)} %copy-done.12), channel_id=1, source_target_pairs={{0,4},{4,0},{1,5},{5,1},{2,6},{6,2},{3,7},{7,3}} | collective-permute-start | bytes 3145736 | tf_op jit(solution)/shard_map/ppermute | solution.py:382
  145.2 42.8 %collective-permute-start.17 = (bf16[256,2048]{1,0:T(8,128)(2,1)}, bf16[256,2048]{1,0:T(8,128)(2,1)}, u32[]{:S(2)}, u32[]{:S(2)}) collective-permute-start(bf16[256,2048]{1,0:T(8,128)(2,1)} %collective-permute-done.15.refs_3_), channel_id=1, source_target_pairs={{0,1},{1,0},{2,3},{3,2},{4,5},{5,4},{6,7},{7,6}} | collective-permute-start | bytes 3145736 | tf_op jit(solution)/shard_map/ppermute | solution.py:383
  145.4 52.0 %collective-permute-start.7 = (bf16[256,2048]{1,0:T(8,128)(2,1)}, bf16[256,2048]{1,0:T(8,128)(2,1)}, u32[]{:S(2)}, u32[]{:S(2)}) collective-permute-start(bf16[256,2048]{1,0:T(8,128)(2,1)} %collective-permute-done.5.refs_3_), channel_id=1, source_target_pairs={{0,1},{1,0},{2,3},{3,2},{4,5},{5,4},{6,7},{7,6}} | collective-permute-start | bytes 3145736 | tf_op jit(solution)/shard_map/ppermute | solution.py:383
  187.9 40.8 %collective-permute-start.21 = (bf16[256,2048]{1,0:T(8,128)(2,1)}, bf16[256,2048]{1,0:T(8,128)(2,1)}, u32[]{:S(2)}, u32[]{:S(2)}) collective-permute-start(bf16[256,2048]{1,0:T(8,128)(2,1)} %copy-done.12), channel_id=1, source_target_pairs={{0,1},{1,0},{2,3},{3,2},{4,5},{5,4},{6,7},{7,6}} | collective-permute-start | bytes 3145736 | tf_op jit(solution)/shard_map/ppermute | solution.py:383
  187.9 40.8 %collective-permute-start.22 = (bf16[256,2048]{1,0:T(8,128)(2,1)}, bf16[256,2048]{1,0:T(8,128)(2,1)}, u32[]{:S(2)}, u32[]{:S(2)}) collective-permute-start(bf16[256,2048]{1,0:T(8,128)(2,1)} %collective-permute-done.20.refs_3_), channel_id=1, source_target_pairs={{0,1},{1,0},{2,3},{3,2},{4,5},{5,4},{6,7},{7,6}} | collective-permute-start | bytes 3145736 | tf_op jit(solution)/shard_map/ppermute | solution.py:383
  228.7 1.3 copy-start.10
  230.0 12.6 %copy-start.7 = (f32[2048,64]{0,1:T(8,128)S(1)}, f32[2048,64]{0,1:T(8,128)}, u32[]{:S(2)}) copy-start(f32[2048,64]{0,1:T(8,128)} %param.15) | copy-start | bytes 1572868
  240.4 2.2 copy-start

commit v3 on v2

--- a/solution.py
+++ b/solution.py
@@ -7,10 +7,6 @@
 from jax.sharding import PartitionSpec as P
 
 EPS = 1e-6
-PAIR = [(0, 1), (1, 0), (2, 3), (3, 2)]
-ACROSS = [(0, 2), (2, 0), (1, 3), (3, 1)]
-SWAP = [(0, 1), (1, 0)]
-VMEM_CAP = 60 * 1024 * 1024
 F32 = jnp.float32
 BF16 = jnp.bfloat16
 
@@ -20,116 +16,229 @@
     return wide * lax.rsqrt(jnp.mean(wide * wide, axis=-1, keepdims=True) + EPS)
 
 
-def params(*semantics):
-    return pltpu.CompilerParams(dimension_semantics=semantics, vmem_limit_bytes=VMEM_CAP)
-
-
-def piece_sum(offs_ref, left_ref, piece_refs):
-    total = None
-    for idx, ref in enumerate(piece_refs):
-        depth = ref.shape[0]
-        cols = pl.ds(pl.multiple_of(offs_ref[idx], depth), depth)
-        part = jnp.dot(left_ref[:, cols], ref[...], preferred_element_type=F32)
-        total = part if total is None else total + part
-    return total
-
-
-def proj_kernel(offs_ref, left_ref, *refs):
-    refs[-1][...] = piece_sum(offs_ref, left_ref, refs[:-1]).astype(BF16)
-
-
-def project(offs, normed, pieces, block=512):
-    rows, depth = normed.shape
-    cols = pieces[0].shape[1]
-    specs = [pl.BlockSpec((piece.shape[0], block), lambda n: (0, n)) for piece in pieces]
+def head_attention(q_ref, k_ref, v_ref, out_ref, lanes, rows, scale):
+    seq = q_ref.shape[0]
+    steps = [slice(start, start + rows) for start in range(0, seq, rows)]
+    keep = lax.broadcasted_iota(jnp.int32, (rows, rows), 0) >= lax.broadcasted_iota(jnp.int32, (rows, rows), 1)
+    nt_dims = (((1,), (1,)), ((), ()))
+    scored = []
+    for step in steps:
+        tile = q_ref[step, lanes]
+        diag = lax.dot_general(tile, k_ref[step, lanes], nt_dims, preferred_element_type=F32)
+        parts = [jnp.where(keep, diag, -jnp.inf)]
+        if step.start:
+            parts.append(lax.dot_general(tile, k_ref[:step.start, lanes], nt_dims, preferred_element_type=F32))
+        scored.append(parts)
+    weighted = []
+    for parts in scored:
+        top = functools.reduce(jnp.maximum, [jnp.max(part, axis=-1, keepdims=True) for part in parts])
+        expo = [jnp.exp((part - top) * scale) for part in parts]
+        total = sum(jnp.sum(part, axis=-1, keepdims=True) for part in expo)
+        inverse = 1.0 / total
+        weighted.append([(part * inverse).astype(BF16) for part in expo])
+    for step, parts in zip(steps, weighted):
+        mixed = jnp.dot(parts[0], v_ref[step, lanes], preferred_element_type=F32)
+        if step.start:
+            mixed += jnp.dot(parts[1], v_ref[:step.start, lanes], preferred_element_type=F32)
+        out_ref[step, lanes] = mixed.astype(BF16)
+
+
+def front_kernel(ids_ref, x_ref, wq_ref, wk_ref, wv_ref, wo_ref, hid_ref, u_ref, pos_ref, oh_ref,
+                 full, normed, qkv, ctx, ids_all, oh_buf,
+                 own_s, po_s, po_r, xs, xr, ys, yr, rs, rr, ids_s, ids_r, oh_s, *, subs, cap, count, head_dim):
+    group, me = lax.axis_index('dp'), lax.axis_index('ep')
+    weights = (wq_ref, wk_ref, wv_ref, wo_ref)
+    shard, model = wo_ref.shape
+    seq = x_ref.shape[0]
+    half, rows, cols = shard // 2, shard // 2 // subs, model // 2
+    order = [(0, 0), (1, 0), (2, 0), (0, 1), (1, 1), (2, 1), (3, 0), (3, 1)]
+    heads = model // head_dim
+
+    def remote(src, dst, send, recv, where):
+        return pltpu.make_async_remote_copy(src_ref=src, dst_ref=dst, send_sem=send, recv_sem=recv,
+                                            device_id=where, device_id_type=pl.DeviceIdType.MESH)
+
+    def block(stage, source, which, sub):
+        matrix, side = order[stage]
+        start = pl.multiple_of(source * shard + which * half + sub * rows, rows)
+        return full.at[matrix, pl.ds(start, rows), pl.ds(side * cols, cols)]
+
+    def own_rows(matrix):
+        return full.at[matrix, pl.ds(pl.multiple_of(me * shard, shard), shard)]
+
+    def own_local(matrix):
+        return pltpu.make_async_copy(weights[matrix], own_rows(matrix), own_s.at[matrix])
+
+    def own_pair(matrix):
+        return remote(weights[matrix], own_rows(matrix), po_s.at[matrix], po_r.at[matrix], {'ep': me ^ 1})
+
+    def x_copy(stage, sub):
+        matrix, side = order[stage]
+        src = weights[matrix].at[pl.ds(pl.multiple_of(group * half + sub * rows, rows), rows), pl.ds(side * cols, cols)]
+        sem = stage * subs + sub
+        return remote(src, block(stage, me, group, sub), xs.at[sem], xr.at[sem], {'ep': me ^ 2})
+
+    def y_copy(stage, sub):
+        ref = block(stage, me ^ 2, group, sub)
+        sem = stage * subs + sub
+        return remote(ref, ref, ys.at[sem], yr.at[sem], {'dp': 1 - group})
+
+    def relay(stage, sub, other):
+        ref = block(stage, me ^ 2, 1 - group if other else group, sub)
+        sem = (stage * subs + sub) * 2 + other
+        return remote(ref, ref, rs.at[sem], rr.at[sem], {'ep': me ^ 1})
+
+    def ids_copy(relation):
+        return remote(ids_ref, ids_all.at[relation - 1], ids_s.at[relation - 1], ids_r.at[relation - 1], {'ep': me ^ relation})
+
+    def oh_copy(source):
+        return pltpu.make_async_copy(oh_buf.at[source % 2], oh_ref.at[source], oh_s.at[source % 2])
+
+    barrier = pltpu.get_barrier_semaphore()
+    for peer in ({'ep': me ^ 1}, {'ep': me ^ 2}, {'ep': me ^ 3}, {'dp': 1 - group}):
+        pl.semaphore_signal(barrier, inc=1, device_id=peer, device_id_type=pl.DeviceIdType.MESH)
+    pl.semaphore_wait(barrier, 4)
+
+    for relation in (1, 2, 3):
+        ids_copy(relation).start()
+    messages = [(stage, sub) for stage in range(len(order)) for sub in range(subs)]
+    for message in messages:
+        x_copy(*message).start()
+    for matrix in range(4):
+        own_pair(matrix).start()
+        own_local(matrix).start()
+
+    normed[...] = rms_norm(x_ref[...]).astype(BF16)
+
+    def place_tokens():
+        for relation in (1, 2, 3):
+            ids_copy(relation).wait_recv()
+        mine = lax.broadcasted_iota(jnp.int32, (count, seq), 0) + me * count
+        earlier = (lax.broadcasted_iota(jnp.int32, (seq, seq), 0) < lax.broadcasted_iota(jnp.int32, (seq, seq), 1))
+        earlier = earlier.astype(F32).astype(BF16)
+        places = []
+        for source in range(4):
+            ids = ids_ref[...] if source == 0 else ids_all[source - 1]
+            member = mine == ids[0:1, :]
+            for choice in range(1, ids.shape[0]):
+                member = jnp.logical_or(member, mine == ids[choice:choice + 1, :])
+            before = jnp.dot(member.astype(F32).astype(BF16), earlier, preferred_element_type=F32)
+            places.append(jnp.where(member, before, -1.0))
+            pos_ref[source] = places[source].astype(jnp.int32)
+        filler = jnp.zeros((128 - 4 * count, seq), F32)
+        by_token = jnp.concatenate(places + [filler], axis=0).T
+        slots = lax.broadcasted_iota(jnp.int32, (seq, cap), 1).astype(F32)
+        for source in range(4):
+            if source >= 2:
+                oh_copy(source - 2).wait()
+            for expert in range(count):
+                lane = source * count + expert
+                hit = by_token[:, lane:lane + 1] == slots
+                oh_buf[source % 2, :, expert * cap:(expert + 1) * cap] = hit.astype(F32).astype(BF16)
+            oh_copy(source).start()
+
+    def ready(stage):
+        matrix, side = order[stage]
+        if side == 0:
+            own_local(matrix).wait()
+            own_pair(matrix).wait_recv()
+        for sub in range(subs):
+            relay(stage, sub, 0).wait_recv()
+            relay(stage, sub, 1).wait_recv()
+
+    def project(stage):
+        matrix, side = order[stage]
+
+        def body(idx, carry):
+            lanes = pl.ds(pl.multiple_of(side * cols + idx * 256, 256), 256)
+            qkv[matrix, :, lanes] = jnp.dot(normed[...], full[matrix, :, lanes], preferred_element_type=F32).astype(BF16)
+            return carry
+        lax.fori_loop(0, cols // 256, body, 0)
+
+    def attend(first, last):
+        def body(head, carry):
+            lanes = pl.ds(pl.multiple_of(head * head_dim, head_dim), head_dim)
+            head_attention(qkv.at[0], qkv.at[1], qkv.at[2], ctx, lanes, 128, head_dim ** -0.5)
+            return carry
+        lax.fori_loop(first, last, body, 0)
+
+    def combine(stage):
+        side = order[stage][1]
+
+        def body(idx, carry):
+            lanes = pl.ds(pl.multiple_of(side * cols + idx * 256, 256), 256)
+            mixed = jnp.dot(ctx[...], full[3, :, lanes], preferred_element_type=F32)
+            hid_ref[:, lanes] = (x_ref[:, lanes].astype(F32) + mixed).astype(BF16)
+            return carry
+        lax.fori_loop(0, cols // 256, body, 0)
+
+    def work(stage, sub):
+        if (stage, sub) == (0, 0):
+            place_tokens()
+        if sub == 0 and stage > 0:
+            ready(stage - 1)
+            if stage - 1 < 6:
+                project(stage - 1)
+        quarter = heads // 8
+        if sub == subs - 1 and 3 <= stage <= 5:
+            first = (0, 3, 6)[stage - 3] * quarter // 2
+            attend(first, min(first + 3 * quarter // 2, heads // 2))
+        if stage == 6:
+            attend(heads // 2 + sub * quarter, heads // 2 + (sub + 1) * quarter)
+        if stage == 7 and sub == 0:
+            attend(heads // 2 + subs * quarter, heads)
+            combine(6)
+
+    previous = None
+    for message in messages:
+        x_copy(*message).wait_recv()
+        y_copy(*message).start()
+        relay(*message, 0).start()
+        if previous is not None:
+            y_copy(*previous).wait_recv()
+            relay(*previous, 1).start()
+        work(*message)
+        previous = message
+    y_copy(*previous).wait_recv()
+    relay(*previous, 1).start()
+    ready(7)
+    combine(7)
+    u_ref[...] = rms_norm(hid_ref[...]).astype(BF16)
+
+    oh_copy(2).wait()
+    oh_copy(3).wait()
+    for relation in (1, 2, 3):
+        ids_copy(relation).wait_send()
+    for matrix in range(4):
+        own_pair(matrix).wait_send()
+    for message in messages:
+        x_copy(*message).wait_send()
+        y_copy(*message).wait_send()
+        relay(*message, 0).wait_send()
+        relay(*message, 1).wait_send()
+
+
+def front(ids_lane, tokens, w_query, w_key, w_value, w_out, cap, count, head_dim):
+    seq, model = tokens.shape
+    subs = 2
+    vmem = pl.BlockSpec(memory_space=pltpu.VMEM)
+    hbm = pl.BlockSpec(memory_space=pl.ANY)
+    dma = pltpu.SemaphoreType.DMA
+    sends = 8 * subs
     return pl.pallas_call(
-        proj_kernel,
-        grid=(cols // block,),
-        in_specs=[pl.BlockSpec(memory_space=pltpu.SMEM), pl.BlockSpec((rows, depth), lambda n: (0, 0))] + specs,
-        out_specs=pl.BlockSpec((rows, block), lambda n: (0, n)),
-        out_shape=jax.ShapeDtypeStruct((rows, cols), BF16),
-        compiler_params=params('arbitrary'),
-        cost_estimate=pl.CostEstimate(flops=2 * rows * depth * cols, bytes_accessed=2 * depth * cols, transcendentals=0),
-        name='project',
-    )(offs, normed, *pieces)
-
-
-def attn_kernel(q_ref, k_ref, v_ref, o_ref, *, rows, scale):
-    seq = q_ref.shape[0]
-    for head in range(q_ref.shape[1] // 128):
-        lanes = slice(head * 128, head * 128 + 128)
-        for start in range(0, seq, rows):
-            stop = start + rows
-            scores = lax.dot_general(q_ref[start:stop, lanes], k_ref[:stop, lanes], (((1,), (1,)), ((), ())),
-                                     preferred_element_type=F32) * scale
-            row_id = lax.broadcasted_iota(jnp.int32, (rows, stop), 0) + start
-            col_id = lax.broadcasted_iota(jnp.int32, (rows, stop), 1)
-            scores = jnp.where(row_id >= col_id, scores, -jnp.inf)
-            top = jnp.max(scores, axis=-1, keepdims=True)
-            expo = jnp.exp(scores - top)
-            weights = (expo / jnp.sum(expo, axis=-1, keepdims=True)).astype(BF16)
-            o_ref[start:stop, lanes] = jnp.dot(weights, v_ref[:stop, lanes], preferred_element_type=F32).astype(BF16)
-
-
-def attend(query, keys, values, head_dim, heads_step=2):
-    seq, width = query.shape
-    block = head_dim * heads_step
-    spec = pl.BlockSpec((seq, block), lambda h: (0, h))
-    return pl.pallas_call(
-        functools.partial(attn_kernel, rows=128, scale=head_dim ** -0.5),
-        grid=(width // block,),
-        in_specs=[spec] * 3,
-        out_specs=spec,
-        out_shape=jax.ShapeDtypeStruct((seq, width), BF16),
-        compiler_params=params('arbitrary'),
-        cost_estimate=pl.CostEstimate(flops=8 * seq * seq * width, bytes_accessed=8 * seq * width, transcendentals=0),
-        name='attend',
-    )(query, keys, values)
-
-
-def out_kernel(offs_ref, left_ref, x_ref, *refs):
-    hidden = (x_ref[...].astype(F32) + piece_sum(offs_ref, left_ref, refs[:-2])).astype(BF16)
-    refs[-2][...] = hidden
-    refs[-1][...] = rms_norm(hidden).astype(BF16)
-
-
-def out_project(offs, context, tokens, pieces, block=256):
-    rows, depth = context.shape
-    cols = pieces[0].shape[1]
-    row_spec = pl.BlockSpec((block, cols), lambda m: (m, 0))
-    return pl.pallas_call(
-        out_kernel,
-        grid=(rows // block,),
-        in_specs=[pl.BlockSpec(memory_space=pltpu.SMEM), pl.BlockSpec((block, depth), lambda m: (m, 0)), row_spec]
-        + [pl.BlockSpec(piece.shape, lambda m: (0, 0)) for piece in pieces],
-        out_specs=[row_spec, row_spec],
-        out_shape=[jax.ShapeDtypeStruct((rows, cols), BF16)] * 2,
-        compiler_params=params('arbitrary'),
-        cost_estimate=pl.CostEstimate(flops=2 * rows * depth * cols, bytes_accessed=2 * depth * cols, transcendentals=0),
-        name='out_project',
-    )(offs, context, tokens, *pieces)
-
-
-def spread_kernel(pos_ref, out_ref):
-    expert = pl.program_id(1)
-    seq = pos_ref.shape[1]
-    lanes = lax.broadcasted_iota(jnp.int32, (seq, pos_ref.shape[2]), 1)
-    place = jnp.sum(jnp.where(lanes == expert, pos_ref[0], 0), axis=-1, keepdims=True)
-    slots = lax.broadcasted_iota(jnp.int32, (seq, out_ref.shape[2]), 1)
-    out_ref[0] = (place == slots).astype(F32).astype(BF16)
-
-
-def spread(pos, cap):
-    sources, seq, count = pos.shape
-    return pl.pallas_call(
-        spread_kernel,
-        grid=(sources, count),
-        in_specs=[pl.BlockSpec((1, seq, count), lambda s, e: (s, 0, 0))],
-        out_specs=pl.BlockSpec((1, seq, cap), lambda s, e: (s, 0, e)),
-        out_shape=jax.ShapeDtypeStruct((sources, seq, count * cap), BF16),
-        compiler_params=params('arbitrary', 'arbitrary'),
-        name='spread',
-    )(pos)
+        functools.partial(front_kernel, subs=subs, cap=cap, count=count, head_dim=head_dim),
+        in_specs=[vmem, vmem, hbm, hbm, hbm, hbm],
+        out_specs=[vmem, vmem, vmem, hbm],
+        out_shape=[jax.ShapeDtypeStruct((seq, model), BF16), jax.ShapeDtypeStruct((seq, model), BF16),
+                   jax.ShapeDtypeStruct((4, count, seq), jnp.int32), jax.ShapeDtypeStruct((4, seq, count * cap), BF16)],
+        scratch_shapes=[
+            pltpu.VMEM((4, model, model), BF16), pltpu.VMEM((seq, model), BF16), pltpu.VMEM((3, seq, model), BF16),
+            pltpu.VMEM((seq, model), BF16), pltpu.VMEM((3,) + ids_lane.shape, jnp.int32), pltpu.VMEM((2, seq, count * cap), BF16),
+            dma((4,)), dma((4,)), dma((4,)), dma((sends,)), dma((sends,)), dma((sends,)), dma((sends,)),
+            dma((2 * sends,)), dma((2 * sends,)), dma((3,)), dma((3,)), dma((2,))],
+        compiler_params=pltpu.CompilerParams(collective_id=2, has_side_effects=True, vmem_limit_bytes=67043328),
+        name='front',
+    )(ids_lane, tokens, w_query, w_key, w_value, w_out)
 
 
 def moe_kernel(pos_ref, u_ref, gate_ref, hid_ref, w1_ref, w3_ref, w2_ref, oh_ref, out_ref,
@@ -192,13 +301,12 @@
     lanes = lax.broadcasted_iota(jnp.int32, (2 * cap, 128), 1)
 
     def up_step(phase, expert):
-        place = pos_ref[expert]
         if phase == 0:
             sources = ((u_ref[...], gate_ref[pl.ds(me * count + expert, 1), :]), (ug[0], gg[0, pl.ds(expert, 1), :]))
         else:
             sources = ((ug[1], gg[1, pl.ds(expert, 1), :]), (ug[2], gg[2, pl.ds(expert, 1), :]))
         for src, (u_val, gate_row) in enumerate(sources):
-            hit = place[2 * phase + src:2 * phase + src + 1, :] == slots
+            hit = pos_ref[2 * phase + src, pl.ds(expert, 1), :] == slots
             rows[src * cap:(src + 1) * cap, :] = jnp.dot(hit.astype(F32).astype(BF16), u_val,
                                                          preferred_element_type=F32).astype(BF16)
             column = jnp.sum(jnp.where(hit, gate_row, 0.0), axis=-1, keepdims=True)
@@ -365,48 +473,12 @@
         experts = w_router.shape[1]
         own_experts = w_one.shape[0]
         cap = 2 * seq * choices // experts
-        group = lax.axis_index('dp')
-        me = lax.axis_index('ep')
-        x_rows = tokens[0]
-        shard = w_out.shape[0]
-        half = shard // 2
-
-        pair = functools.partial(lax.ppermute, axis_name='ep', perm=PAIR)
-        across = functools.partial(lax.ppermute, axis_name='ep', perm=ACROSS)
-        swap = functools.partial(lax.ppermute, axis_name='dp', perm=SWAP)
-
-        def gather(weight):
-            mine = lax.dynamic_slice_in_dim(weight, group * half, half, 0).reshape(half, -1)
-            full = weight.reshape(shard, -1)
-            far = across(mine)
-            far_other = swap(far)
-            return [full, pair(full), far, far_other, pair(far), pair(far_other)]
-
-        offs = jnp.stack([me * shard, (me ^ 1) * shard,
-                          (me ^ 2) * shard + group * half, (me ^ 2) * shard + (1 - group) * half,
-                          (me ^ 3) * shard + group * half, (me ^ 3) * shard + (1 - group) * half]).astype(jnp.int32)
-        q_parts, k_parts, v_parts, o_parts = [gather(w) for w in (w_query, w_key, w_value, w_out)]
-
         ids = expert_ids[0]
-        ids_pair = pair(ids)
-        ids_far = across(ids)
-        ids_all = jnp.stack([ids, ids_pair, ids_far, pair(ids_far)])
-        mine = me * own_experts + jnp.arange(own_experts, dtype=jnp.int32)
-        member = jnp.any(ids_all[:, :, :, None] == mine, axis=2)
-        count = member.astype(jnp.int32)
-        pos = jnp.where(member, jnp.cumsum(count, axis=1) - count, -1)
-        pos_lane = pos.transpose(2, 0, 1)
-
-        normed = rms_norm(x_rows).astype(BF16)
-        query = project(offs, normed, q_parts)
-        keys = project(offs, normed, k_parts)
-        values = project(offs, normed, v_parts)
-        context = attend(query, keys, values, head_dim)
-        hidden, u_own = out_project(offs, context, x_rows, o_parts)
-
+        flat = [w.reshape(w.shape[0], -1) for w in (w_query, w_key, w_value)]
+        hidden, u_own, pos, onehot = front(ids.T, tokens[0], *flat, w_out, cap, own_experts, head_dim)
         logits = jnp.dot(rms_norm(hidden), w_router, precision=lax.Precision.HIGHEST, preferred_element_type=F32)
         chosen = jnp.any(ids[:, :, None] == jnp.arange(experts, dtype=jnp.int32), axis=1)
         gates = jax.nn.softmax(jnp.where(chosen, logits, -jnp.inf), axis=-1)
-        return moe(pos_lane, u_own, gates.T, hidden, w_one, w_three, w_two, spread(pos, cap), cap)[None]
+        return moe(pos, u_own, gates.T, hidden, w_one, w_three, w_two, onehot, cap)[None]
 
     return jax.shard_map(local_layer, mesh=mesh, in_specs=(tok_spec, row_spec, row_spec, row_spec, row_spec, P(), row_spec, row_spec, row_spec, tok_spec), out_specs=tok_spec, check_vma=False)

time: 494 us -> 386 us (0.78)
  waiting for transfers between devices: 114 us -> 0 us
  Pallas kernels: 328 us -> 359 us
  starting transfers between devices: 14.6 us -> 0 us
  other arithmetic: 11.3 us -> 3.82 us
    ppermute x23 -> x0, waiting for transfers between devices: 114 us -> none  [the longest x1 42.2 us: local_layer(): ids_far = across(ids)]
    pallas_call x6 -> x1, Pallas kernels: 90.5 us -> 121 us  [front(): pl.pallas_call(functools.partial(front_kernel, subs=subs, cap=cap, count=...]
    ppermute x23 -> x0, starting transfers between devices: 14.6 us -> none  [the longest x4 5.44 us: gather(): far = across(mine)]
    reshape x0 -> x1, local copies, waits for them, and re-layouts: none -> 6.44 us  [local_layer(): flat = [w.reshape(w.shape[0], -1) for w in (w_query, w_key, w_value)]]
    unnamed x39 -> x6, local copies, waits for them, and re-layouts: 11.1 us -> 5.03 us
    another operation x5 -> x0, other arithmetic: 5.02 us -> none
  transfers between devices with their start and end apart: 23 -> 0, of which waited for: 6 -> 0; matrix products, arithmetic and copies ran while one was open for 3% -> 0% of each run, Pallas kernels for 16% -> 0%
where the time goes in v3:
time: 386 us; the launch traced here: 380 us
  Pallas kernels  359 us (93%)
  local copies, waits for them, and re-layouts  11.5 us (3%)
  matrix products  5.5 us (1%)
    pallas_call x1, Pallas kernels, moe(): pl.pallas_call(functools.partial(moe_kernel, cap=cap, u_chunks=u_chunks,...  238 us
    pallas_call x1, Pallas kernels, front(): pl.pallas_call(functools.partial(front_kernel, subs=subs, cap=cap, count=...  121 us

profile of v3, /device:TPU:0, one launch (start us, length us, event | category | flops | bytes accessed | tf_op | source)
XLA Modules:
  0.0 379.9 jit_solution(4855621437334490416)
XLA Ops:
  0.0 0.0 copy-start.1
  0.0 6.4 %copy_bitcast_fusion = (bf16[512,2048]{1,0:T(8,128)(2,1)}, bf16[512,2048]{1,0:T(8,128)(2,1)}) fusion(bf16[64,8,16,128]{3,2,1,0:T(8,128)(2,1)} %bitcast.22, bf16[64,8,16,128]{3,2,1,0:T(8,128)(2,1)} %bitcast.23), kind=kLoop, calls=%fused_computation.4 | loop fusion | bytes 8388608 | tf_op jit(solution)/shard_map/reshape | solution.py:477
  6.4 0.0 copy-done.1
  6.4 1.9 copy.18
  8.3 120.9 %front.1 = (bf16[512,2048]{1,0:T(8,128)(2,1)}, bf16[512,2048]{1,0:T(8,128)(2,1)}, s32[4,16,512]{2,1,0:T(8,128)}, bf16[4,512,2048]{2,1,0:T(8,128)(2,1)}) custom-call(s32[8,512]{1,0:T(8,128)} %bitcast.24, bf16[512,2048]{1,0:T(8,128)(2,1)} %bitcast.20, bf16[512,2048]{1,0:T(8,128)(2,1)} %bitcast.19, bf16[512,2048]{1,0:T(8,128)(2,1)} %get-tuple-element.16.wk_ref, ...), custom_call_target="tpu_custom_call" | custom-call | tf_op jit(solution)/shard_map/front/pallas_call | solution.py:228
  129.2 0.0 copy-start
  129.2 2.2 fusion
  131.5 0.9 fusion.4
  132.3 0.0 copy-done
  132.3 5.5 %fusion.6 = (f32[512]{0:T(512)S(1)}, f32[512,64]{0,1:T(8,128)S(1)}) fusion(pred[512,64]{0,1:T(8,128)(4,1)S(1)} %fusion.4, f32[2048,64]{0,1:T(8,128)} %param.15, bf16[512,2048]{1,0:T(8,128)(2,1)S(1)} %copy-done, f32[512]{0:T(512)S(1)} %add_rsqrt_fusion), kind=kOutput, calls=%fused_computation.15 | convolution fusion | flops 807468544 | bytes 2789376 | tf_op jit(solution)/shard_map/dot_general | solution.py:479
  137.9 0.7 divide_bitcast_fusion.gate_ref
  138.6 237.7 %moe.1 = bf16[512,2048]{1,0:T(8,128)(2,1)} custom-call(s32[4,16,512]{2,1,0:T(8,128)} %get-tuple-element.9.pos_ref, bf16[512,2048]{1,0:T(8,128)(2,1)} %get-tuple-element.10.u_ref, f32[64,512]{1,0:T(8,128)} %divide_bitcast_fusion.gate_ref, bf16[512,2048]{1,0:T(8,128)(2,1)} %get-tuple-element.11.hid_ref, bf16[16,2048,1024]{2,1,0:T(8,128)(2,1)} %w1_ref.1, ...), custom_call_target="tpu_custom_call" | custom-call | tf_op jit(solution)/shard_map/moe/pallas_call | solution.py:446
  376.3 3.2 copy.20
  (2 shorter events, 0.1 us)
Async XLA Ops:
  0.0 6.4 %copy-start.1 = (bf16[512,16,128]{2,1,0:T(8,128)(2,1)S(1)}, bf16[512,16,128]{2,1,0:T(8,128)(2,1)}, u32[]{:S(2)}) copy-start(bf16[512,16,128]{2,1,0:T(8,128)(2,1)} %param.11) | copy-start | bytes 6291460
  129.2 3.1 copy-start

commit v4 on v3

--- a/solution.py
+++ b/solution.py
@@ -220,7 +220,7 @@
 
 def front(ids_lane, tokens, w_query, w_key, w_value, w_out, cap, count, head_dim):
     seq, model = tokens.shape
-    subs = 2
+    subs = 4
     vmem = pl.BlockSpec(memory_space=pltpu.VMEM)
     hbm = pl.BlockSpec(memory_space=pl.ANY)
     dma = pltpu.SemaphoreType.DMA
@@ -242,8 +242,8 @@
 
 
 def moe_kernel(pos_ref, u_ref, gate_ref, hid_ref, w1_ref, w3_ref, w2_ref, oh_ref, out_ref,
-               ug, gg, rows, act, gcol, w13, w2t, oht, pst, acc, pair_buf, far_src, far_dst,
-               us, ur, gs, gr, ws, w2s, ohs, ps, pr, xs, xr,
+               ug, gg, rows, act, gcol, pool, oht, pst, acc, pair_buf, far_src, far_dst,
+               us, ur, gs, gr, ws, ohs, ps, pr, xs, xr,
                *, cap, u_chunks, chunks, groups, wslots):
     me = lax.axis_index('ep')
     relations = (me ^ 1, me ^ 2, me ^ 3)
@@ -258,21 +258,39 @@
         return pltpu.make_async_remote_copy(src_ref=src, dst_ref=dst, send_sem=send, recv_sem=recv,
                                             device_id={'ep': relations[relation]}, device_id_type=pl.DeviceIdType.MESH)
 
-    def w13_copy(expert, slot, which):
-        ref = (w1_ref, w3_ref)[which]
-        return pltpu.make_async_copy(ref.at[expert, :, pl.ds(slot * col, col)], w13.at[slot, which], ws.at[slot, which])
-
-    def w2_copy(chunk, part, slot):
-        return pltpu.make_async_copy(w2_ref.at[pl.ds(part * per, per), :, pl.ds(pl.multiple_of(chunk * block, block), block)],
-                                     w2t.at[slot], w2s.at[slot])
-
-    def oh_copy(phase, part, slot):
-        return pltpu.make_async_copy(oh_ref.at[pl.ds(2 * phase, 2), :, pl.ds(part * per * cap, per * cap)],
+    ring = pool.shape[0]
+    up_tiles = 2 * count * wslots
+
+    def w13_copies(tile):
+        slot, expert = lax.rem(tile, ring), lax.rem(tile // wslots, count)
+        at = pl.multiple_of(lax.rem(tile, wslots) * col, col)
+        return [pltpu.make_async_copy(ref.at[expert, :, pl.ds(at, col)], pool.at[slot, :, pl.ds(which * col, col)], ws.at[slot, which])
+                for which, ref in enumerate((w1_ref, w3_ref))]
+
+    def w2_copies(step):
+        slot = lax.rem(step + up_tiles, ring)
+        at = pl.multiple_of(lax.rem(step // groups, chunks) * block, block)
+        return [pltpu.make_async_copy(w2_ref.at[lax.rem(step, groups) * per + idx, :, pl.ds(at, block)],
+                                      pool.at[slot, pl.ds(idx * width, width), :], ws.at[slot, idx]) for idx in range(per)]
+
+    def w13_start(tile):
+        for copy in w13_copies(tile):
+            copy.start()
+
+    def w2_start(step):
+        for copy in w2_copies(step):
+            copy.start()
+
+    def oh_copy(step):
+        slot = lax.rem(step, 3)
+        phase = 1 - step // (groups * chunks)
+        depth = per * cap
+        return pltpu.make_async_copy(oh_ref.at[pl.ds(2 * phase, 2), :,
+                                               pl.ds(pl.multiple_of(lax.rem(step, groups) * depth, depth), depth)],
                                      oht.at[slot], ohs.at[slot])
 
-    for slot in range(wslots):
-        w13_copy(0, slot, 0).start()
-        w13_copy(0, slot, 1).start()
+    for tile in range(ring):
+        w13_start(tile)
 
     barrier = pltpu.get_barrier_semaphore()
     for peer in relations:
@@ -284,11 +302,11 @@
     pair_send = remote(u_ref, ug.at[0], us.at[0], ur.at[0], 0)
 
     def far_send(idx):
-        part = pl.ds(idx * piece, piece)
+        part = pl.ds(pl.multiple_of(idx * piece, piece), piece)
         return remote(u_ref.at[part], ug.at[1, part], us.at[1 + idx], ur.at[1 + idx], 1)
 
     def relay_send(idx):
-        part = pl.ds(idx * piece, piece)
+        part = pl.ds(pl.multiple_of(idx * piece, piece), piece)
         return remote(ug.at[1, part], ug.at[2, part], us.at[1 + u_chunks + idx], ur.at[1 + u_chunks + idx], 0)
 
     for send in gate_sends:
@@ -298,132 +316,169 @@
     pair_send.start()
 
     slots = lax.broadcasted_iota(jnp.int32, (cap, seq), 0)
-    lanes = lax.broadcasted_iota(jnp.int32, (2 * cap, 128), 1)
-
-    def up_step(phase, expert):
+    lanes = lax.broadcasted_iota(jnp.int32, (cap, 128), 1)
+
+    def up_step(phase, index):
+        first_expert = 2 * index
+        first_tile = (phase * count + first_expert) * wslots
         if phase == 0:
-            sources = ((u_ref[...], gate_ref[pl.ds(me * count + expert, 1), :]), (ug[0], gg[0, pl.ds(expert, 1), :]))
+            sources = ((u_ref, gate_ref, me * count), (ug.at[0], gg.at[0], 0))
         else:
-            sources = ((ug[1], gg[1, pl.ds(expert, 1), :]), (ug[2], gg[2, pl.ds(expert, 1), :]))
-        for src, (u_val, gate_row) in enumerate(sources):
-            hit = pos_ref[2 * phase + src, pl.ds(expert, 1), :] == slots
-            rows[src * cap:(src + 1) * cap, :] = jnp.dot(hit.astype(F32).astype(BF16), u_val,
-                                                         preferred_element_type=F32).astype(BF16)
-            column = jnp.sum(jnp.where(hit, gate_row, 0.0), axis=-1, keepdims=True)
-            part = slice(src * cap, (src + 1) * cap)
-            gcol[phase, part, :] = jnp.where(lanes[part] == expert, column, gcol[phase, part, :])
-        for slot in range(wslots):
-            w13_copy(0, slot, 0).wait()
-            w13_copy(0, slot, 1).wait()
-            first = jnp.dot(rows[...], w13[slot, 0], preferred_element_type=F32)
-            third = jnp.dot(rows[...], w13[slot, 1], preferred_element_type=F32)
-            act[phase * count + expert, :, slot * col:(slot + 1) * col] = (jax.nn.silu(first) * third).astype(BF16)
-
-            def refill(slot=slot):
-                following = lax.rem(expert + 1, count)
-                w13_copy(following, slot, 0).start()
-                w13_copy(following, slot, 1).start()
-
-            if phase == 0:
-                refill()
-            else:
-                pl.when(expert < count - 1)(refill)
+            sources = ((ug.at[1], gg.at[1], 0), (ug.at[2], gg.at[2], 0))
+
+        def gather():
+            for src, (tokens_ref, gates_ref, offset) in enumerate(sources):
+                part = slice(src * cap, (src + 1) * cap)
+                picks = []
+                for idx in range(2):
+                    hit = pos_ref[2 * phase + src, pl.ds(first_expert + idx, 1), :] == slots
+                    picks.append(hit.astype(F32).astype(BF16))
+                    gate_row = gates_ref[pl.ds(offset + first_expert + idx, 1), :]
+                    column = jnp.sum(jnp.where(hit, gate_row, 0.0), axis=-1, keepdims=True)
+                    gcol[phase, part, :] = jnp.where(lanes == first_expert + idx, column, gcol[phase, part, :])
+                picked = jnp.dot(jnp.concatenate(picks, axis=0), tokens_ref[...], preferred_element_type=F32).astype(BF16)
+                rows[0, part, :] = picked[:cap]
+                rows[1, part, :] = picked[cap:]
+
+        def finish(expert, slot, both):
+            act[phase * count + expert, :, slot * col:(slot + 1) * col] = (jax.nn.silu(both[:, :col]) * both[:, col:]).astype(BF16)
+
+        for start in range(0, 2 * wslots, 2):
+            for tile in (start, start + 1):
+                for copy in w13_copies(first_tile + tile):
+                    copy.wait()
+            if start == 0:
+                gather()
+            results = []
+            for tile in (start, start + 1):
+                idx, slot = divmod(tile, wslots)
+                results.append((first_expert + idx, slot,
+                                jnp.dot(rows[idx], pool[lax.rem(first_tile + tile, ring)], preferred_element_type=F32)))
+            for result in results:
+                finish(*result)
+            for tile in (start, start + 1):
+                ahead = first_tile + tile + ring
+                if phase == 0:
+                    w13_start(ahead)
+                else:
+                    @pl.when(ahead < up_tiles)
+                    def _(ahead=ahead):
+                        w13_start(ahead)
+
+                    @pl.when(ahead >= up_tiles)
+                    def _(ahead=ahead):
+                        w2_start(ahead - up_tiles)
 
     gcol[...] = jnp.zeros_like(gcol)
     gate_sends[0].wait_recv()
     pair_send.wait_recv()
-    step = count // u_chunks
-    for idx in range(u_chunks):
-        def near(expert, carry):
-            up_step(0, expert)
-            return carry
-        lax.fori_loop(idx * step, (idx + 1) * step, near, 0)
-        far_send(idx).wait_recv()
-        relay_send(idx).start()
-    for idx in range(3):
-        w2_copy(0, idx, idx).start()
-        oh_copy(1, idx, idx).start()
+    stride = count // 2 // u_chunks
+
+    def near(index, carry):
+        up_step(0, index)
+
+        @pl.when(lax.rem(index, stride) == stride - 1)
+        def _():
+            far_send(index // stride).wait_recv()
+            relay_send(index // stride).start()
+        return carry
+    lax.fori_loop(0, count // 2, near, 0)
+    for idx in range(2):
+        oh_copy(idx).start()
     gate_sends[1].wait_recv()
     gate_sends[2].wait_recv()
     for idx in range(u_chunks):
         relay_send(idx).wait_recv()
 
-    def away(expert, carry):
-        up_step(1, expert)
+    def away(index, carry):
+        up_step(1, index)
         return carry
-    lax.fori_loop(0, count, away, 0)
-
-    def down_chunk(phase, chunk):
-        order = (1 - phase) * chunks + chunk
+    lax.fori_loop(0, count // 2, away, 0)
+
+    total_steps = 2 * chunks * groups
+
+    def pair_sum(order):
+        slot = lax.rem(order, 2)
+        return remote(acc.at[slot, 1], pair_buf.at[slot], ps.at[slot], pr.at[slot], 0)
+
+    def far_sum(chunk):
+        return remote(far_src.at[lax.rem(chunk, 3)], far_dst.at[chunk], xs.at[lax.rem(chunk, 3)], xr.at[chunk], 1)
+
+    def mix(step, order, part):
+        slot = lax.rem(step, 3)
+        for src in range(2):
+            hits = jnp.concatenate([oht[slot, src]] * 3, axis=1)
+            mixed = jnp.dot(hits, pst[part % 2, src], preferred_element_type=F32)
+            if part == 0:
+                acc[lax.rem(order, 2), src] = mixed
+            else:
+                acc[lax.rem(order, 2), src] += mixed
+
+    def settle(order):
+        pair_sum(order).wait_recv()
+        pair_sum(order).wait_send()
+        slot = lax.rem(order, 2)
+
+        @pl.when(order < chunks)
+        def _():
+            @pl.when(order == 3)
+            def _():
+                far_sum(0).wait_send()
+            far_src[lax.rem(order, 3)] = acc[slot, 0] + pair_buf[slot]
+            far_sum(order).start()
+
+        @pl.when(order >= chunks)
+        def _():
+            chunk = order - chunks
+            far_sum(chunk).wait_recv()
+            cols = pl.ds(pl.multiple_of(chunk * block, block), block)
+            total = acc[slot, 0] + pair_buf[slot]
+            out_ref[:, cols] = (hid_ref[:, cols].astype(F32) + total + far_dst[chunk]).astype(BF16)
+
+    def down(order, carry):
+        phase = 1 - order // chunks
         for part in range(groups):
-            slot = lax.rem(order * groups + part, 3)
-            w2_copy(0, 0, slot).wait()
-            oh_copy(0, 0, slot).wait()
+            step = order * groups + part
+            slot = lax.rem(step + up_tiles, ring)
+            for copy in w2_copies(step):
+                copy.wait()
+            oh_copy(step).wait()
             for idx in range(per):
                 expert = part * per + idx
-                done = jnp.dot(act[phase * count + expert], w2t[slot, idx], preferred_element_type=F32).astype(BF16)
+                done = jnp.dot(act[phase * count + expert], pool[slot, idx * width:(idx + 1) * width, :], preferred_element_type=F32).astype(BF16)
                 rest = done.astype(F32) * gcol[phase, :, expert:expert + 1]
                 for term in range(3):
                     head = rest.astype(BF16)
                     at = (term * per + idx) * cap
-                    pst[0, at:at + cap, :] = head[:cap]
-                    pst[1, at:at + cap, :] = head[cap:]
+                    pst[part % 2, 0, at:at + cap, :] = head[:cap]
+                    pst[part % 2, 1, at:at + cap, :] = head[cap:]
                     rest = rest - head.astype(F32)
-            depth = per * cap
-            for src in range(2):
-                mixed = jnp.dot(oht[slot, src], pst[src, 0:depth, :], preferred_element_type=F32)
-                for term in range(1, 3):
-                    mixed += jnp.dot(oht[slot, src], pst[src, term * depth:(term + 1) * depth, :], preferred_element_type=F32)
-                if part == 0:
-                    acc[lax.rem(chunk, 2), src] = mixed
-                else:
-                    acc[lax.rem(chunk, 2), src] += mixed
-
-            def refill(part=part, slot=slot):
-                ahead = order * groups + part + 3
-                ahead_chunk = lax.rem(ahead // groups, chunks)
-                ahead_part = lax.rem(ahead, groups)
-                ahead_phase = 1 - ahead // (groups * chunks)
-                w2_copy(ahead_chunk, ahead_part, slot).start()
-                oh_copy(ahead_phase, ahead_part, slot).start()
-
-            if phase == 1:
-                refill()
+            if part > 0:
+                mix(step - 1, order, part - 1)
             else:
-                pl.when(order * groups + part + 3 < 2 * groups * chunks)(refill)
-
-    def pair_sum(phase, chunk):
-        slot = lax.rem((1 - phase) * chunks + chunk, 4)
-        return remote(acc.at[lax.rem(chunk, 2), 1], pair_buf.at[slot], ps.at[slot], pr.at[slot], 0)
-
-    def far_sum(chunk):
-        return remote(far_src.at[chunk], far_dst.at[chunk], xs.at[chunk], xr.at[chunk], 1)
-
-    def settle(phase, chunk):
-        pair_sum(phase, chunk).wait_recv()
-        pair_sum(phase, chunk).wait_send()
-        slot = lax.rem((1 - phase) * chunks + chunk, 4)
-        total = acc[lax.rem(chunk, 2), 0] + pair_buf[slot]
-        if phase == 1:
-            far_src[chunk] = total
-            far_sum(chunk).start()
-        else:
-            far_sum(chunk).wait_recv()
-            cols = pl.ds(pl.multiple_of(chunk * block, block), block)
-            out_ref[:, cols] = (hid_ref[:, cols].astype(F32) + total + far_dst[chunk]).astype(BF16)
-
-    for phase in (1, 0):
-        def down(chunk, carry, phase=phase):
-            down_chunk(phase, chunk)
-
-            @pl.when(chunk > 0)
+                @pl.when(order > 0)
+                def _():
+                    mix(step - 1, order - 1, groups - 1)
+                    pair_sum(order - 1).start()
+
+            @pl.when(step + ring < total_steps)
             def _():
-                settle(phase, chunk - 1)
-
-            pair_sum(phase, chunk).start()
-            return carry
-        lax.fori_loop(0, chunks, down, 0)
-        settle(phase, chunks - 1)
+                w2_start(step + ring)
+
+            @pl.when(step + 2 < total_steps)
+            def _():
+                oh_copy(step + 2).start()
+
+            if part == 3:
+                @pl.when(order > 0)
+                def _():
+                    settle(order - 1)
+        return carry
+    lax.fori_loop(0, 2 * chunks, down, 0)
+    last = 2 * chunks - 1
+    mix(total_steps - 1, last, groups - 1)
+    pair_sum(last).start()
+    settle(last)
 
     for send in gate_sends:
         send.wait_send()
@@ -431,14 +486,14 @@
     for idx in range(u_chunks):
         far_send(idx).wait_send()
         relay_send(idx).wait_send()
-    for idx in range(chunks):
+    for idx in range(1, chunks):
         far_sum(idx).wait_send()
 
 
 def moe(pos_lane, u_own, gates_lane, hidden, w_one, w_three, w_two, onehot, cap):
     seq, model = u_own.shape
     count, _, width = w_one.shape
-    u_chunks, chunks, groups, wslots = 4, 8, 4, 4
+    u_chunks, chunks, groups, wslots = 4, 4, 8, 4
     block, per = model // chunks, count // groups
     vmem = pl.BlockSpec(memory_space=pltpu.VMEM)
     hbm = pl.BlockSpec(memory_space=pl.ANY)
@@ -449,14 +504,14 @@
         out_specs=vmem,
         out_shape=jax.ShapeDtypeStruct((seq, model), BF16),
         scratch_shapes=[
-            pltpu.VMEM((3, seq, model), BF16), pltpu.VMEM((3, count, seq), F32), pltpu.VMEM((2 * cap, model), BF16),
+            pltpu.VMEM((3, seq, model), BF16), pltpu.VMEM((3, count, seq), F32), pltpu.VMEM((2, 2 * cap, model), BF16),
             pltpu.VMEM((2 * count, 2 * cap, width), BF16), pltpu.VMEM((2, 2 * cap, 128), F32),
-            pltpu.VMEM((wslots, 2, model, width // wslots), BF16), pltpu.VMEM((3, per, width, block), BF16),
-            pltpu.VMEM((3, 2, seq, per * cap), BF16), pltpu.VMEM((2, 3 * per * cap, block), BF16),
-            pltpu.VMEM((2, 2, seq, block), F32), pltpu.VMEM((4, seq, block), F32),
-            pltpu.VMEM((chunks, seq, block), F32), pltpu.VMEM((chunks, seq, block), F32),
-            dma((1 + 2 * u_chunks,)), dma((1 + 2 * u_chunks,)), dma((3,)), dma((3,)), dma((wslots, 2)), dma((3,)), dma((3,)),
-            dma((4,)), dma((4,)), dma((chunks,)), dma((chunks,))],
+            pltpu.VMEM((6, model, block), BF16),
+            pltpu.VMEM((3, 2, seq, per * cap), BF16), pltpu.VMEM((2, 2, 3 * per * cap, block), BF16),
+            pltpu.VMEM((2, 2, seq, block), F32), pltpu.VMEM((2, seq, block), F32),
+            pltpu.VMEM((3, seq, block), F32), pltpu.VMEM((chunks, seq, block), F32),
+            dma((1 + 2 * u_chunks,)), dma((1 + 2 * u_chunks,)), dma((3,)), dma((3,)), dma((6, 2)), dma((3,)),
+            dma((2,)), dma((2,)), dma((3,)), dma((chunks,))],
         compiler_params=pltpu.CompilerParams(collective_id=1, has_side_effects=True, vmem_limit_bytes=67043328),
         name='moe',
     )(pos_lane, u_own, gates_lane, hidden, w_one, w_three, w_two, onehot)

time: 386 us -> 389 us (level)
    pallas_call x1, Pallas kernels: 121 us -> 139 us  [front(): pl.pallas_call(functools.partial(front_kernel, subs=subs, cap=cap, count=...]
    pallas_call x1, Pallas kernels: 238 us -> 222 us  [moe(): pl.pallas_call(functools.partial(moe_kernel, cap=cap, u_chunks=u_chunks,...]
where the time goes in v4:
time: 389 us; the launch traced here: 382 us
  Pallas kernels  361 us (93%)
  local copies, waits for them, and re-layouts  11.5 us (3%)
  matrix products  5.5 us (1%)
    pallas_call x1, Pallas kernels, moe(): pl.pallas_call(functools.partial(moe_kernel, cap=cap, u_chunks=u_chunks,...  222 us
    pallas_call x1, Pallas kernels, front(): pl.pallas_call(functools.partial(front_kernel, subs=subs, cap=cap, count=...  139 us

profile of v4, /device:TPU:0, one launch (start us, length us, event | category | flops | bytes accessed | tf_op | source)
XLA Modules:
  0.0 382.1 jit_solution(15346786068506449847)
XLA Ops:
  0.0 0.0 copy-start.1
  0.0 6.4 %copy_bitcast_fusion = (bf16[512,2048]{1,0:T(8,128)(2,1)}, bf16[512,2048]{1,0:T(8,128)(2,1)}) fusion(bf16[64,8,16,128]{3,2,1,0:T(8,128)(2,1)} %bitcast.22, bf16[64,8,16,128]{3,2,1,0:T(8,128)(2,1)} %bitcast.23), kind=kLoop, calls=%fused_computation.4 | loop fusion | bytes 8388608 | tf_op jit(solution)/shard_map/reshape | solution.py:532
  6.4 0.0 copy-done.1
  6.4 1.9 copy.18
  8.3 139.0 %front.1 = (bf16[512,2048]{1,0:T(8,128)(2,1)}, bf16[512,2048]{1,0:T(8,128)(2,1)}, s32[4,16,512]{2,1,0:T(8,128)}, bf16[4,512,2048]{2,1,0:T(8,128)(2,1)}) custom-call(s32[8,512]{1,0:T(8,128)} %bitcast.24, bf16[512,2048]{1,0:T(8,128)(2,1)} %bitcast.20, bf16[512,2048]{1,0:T(8,128)(2,1)} %bitcast.19, bf16[512,2048]{1,0:T(8,128)(2,1)} %get-tuple-element.16.wk_ref, ...), custom_call_target="tpu_custom_call" | custom-call | tf_op jit(solution)/shard_map/front/pallas_call | solution.py:228
  147.3 0.0 copy-start
  147.3 2.2 fusion
  149.5 0.9 fusion.4
  150.4 0.0 copy-done
  150.4 5.5 %fusion.6 = (f32[512]{0:T(512)S(1)}, f32[512,64]{0,1:T(8,128)S(1)}) fusion(pred[512,64]{0,1:T(8,128)(4,1)S(1)} %fusion.4, f32[2048,64]{0,1:T(8,128)} %param.15, bf16[512,2048]{1,0:T(8,128)(2,1)S(1)} %copy-done, f32[512]{0:T(512)S(1)} %add_rsqrt_fusion), kind=kOutput, calls=%fused_computation.15 | convolution fusion | flops 807468544 | bytes 2789376 | tf_op jit(solution)/shard_map/dot_general | solution.py:534
  156.0 0.7 divide_bitcast_fusion.gate_ref
  156.7 221.8 %moe.1 = bf16[512,2048]{1,0:T(8,128)(2,1)} custom-call(s32[4,16,512]{2,1,0:T(8,128)} %get-tuple-element.9.pos_ref, bf16[512,2048]{1,0:T(8,128)(2,1)} %get-tuple-element.10.u_ref, f32[64,512]{1,0:T(8,128)} %divide_bitcast_fusion.gate_ref, bf16[512,2048]{1,0:T(8,128)(2,1)} %get-tuple-element.11.hid_ref, bf16[16,2048,1024]{2,1,0:T(8,128)(2,1)} %w1_ref.1, ...), custom_call_target="tpu_custom_call" | custom-call | tf_op jit(solution)/shard_map/moe/pallas_call | solution.py:501
  378.5 3.2 copy.20
  (2 shorter events, 0.1 us)
Async XLA Ops:
  0.0 6.4 %copy-start.1 = (bf16[512,16,128]{2,1,0:T(8,128)(2,1)S(1)}, bf16[512,16,128]{2,1,0:T(8,128)(2,1)}, u32[]{:S(2)}) copy-start(bf16[512,16,128]{2,1,0:T(8,128)(2,1)} %param.11) | copy-start | bytes 6291460
  147.3 3.1 copy-start

commit v5 on v4

--- a/solution.py
+++ b/solution.py
@@ -43,14 +43,14 @@
         out_ref[step, lanes] = mixed.astype(BF16)
 
 
-def front_kernel(ids_ref, x_ref, wq_ref, wk_ref, wv_ref, wo_ref, hid_ref, u_ref, pos_ref, oh_ref,
+def front_kernel(ids_ref, x_ref, wr_ref, wq_ref, wk_ref, wv_ref, wo_ref, hid_ref, u_ref, pos_ref, gate_ref, oh_ref,
                  full, normed, qkv, ctx, ids_all, oh_buf,
                  own_s, po_s, po_r, xs, xr, ys, yr, rs, rr, ids_s, ids_r, oh_s, *, subs, cap, count, head_dim):
     group, me = lax.axis_index('dp'), lax.axis_index('ep')
     weights = (wq_ref, wk_ref, wv_ref, wo_ref)
     shard, model = wo_ref.shape
     seq = x_ref.shape[0]
-    half, rows, cols = shard // 2, shard // 2 // subs, model // 2
+    half, cols = shard // 2, model // 2
     order = [(0, 0), (1, 0), (2, 0), (0, 1), (1, 1), (2, 1), (3, 0), (3, 1)]
     heads = model // head_dim
 
@@ -60,6 +60,7 @@
 
     def block(stage, source, which, sub):
         matrix, side = order[stage]
+        rows = half // subs[stage]
         start = pl.multiple_of(source * shard + which * half + sub * rows, rows)
         return full.at[matrix, pl.ds(start, rows), pl.ds(side * cols, cols)]
 
@@ -74,18 +75,19 @@
 
     def x_copy(stage, sub):
         matrix, side = order[stage]
+        rows = half // subs[stage]
         src = weights[matrix].at[pl.ds(pl.multiple_of(group * half + sub * rows, rows), rows), pl.ds(side * cols, cols)]
-        sem = stage * subs + sub
+        sem = sum(subs[:stage]) + sub
         return remote(src, block(stage, me, group, sub), xs.at[sem], xr.at[sem], {'ep': me ^ 2})
 
     def y_copy(stage, sub):
         ref = block(stage, me ^ 2, group, sub)
-        sem = stage * subs + sub
+        sem = sum(subs[:stage]) + sub
         return remote(ref, ref, ys.at[sem], yr.at[sem], {'dp': 1 - group})
 
     def relay(stage, sub, other):
         ref = block(stage, me ^ 2, 1 - group if other else group, sub)
-        sem = (stage * subs + sub) * 2 + other
+        sem = (sum(subs[:stage]) + sub) * 2 + other
         return remote(ref, ref, rs.at[sem], rr.at[sem], {'ep': me ^ 1})
 
     def ids_copy(relation):
@@ -101,7 +103,7 @@
 
     for relation in (1, 2, 3):
         ids_copy(relation).start()
-    messages = [(stage, sub) for stage in range(len(order)) for sub in range(subs)]
+    messages = [(stage, sub) for stage in range(len(order)) for sub in range(subs[stage])]
     for message in messages:
         x_copy(*message).start()
     for matrix in range(4):
@@ -142,7 +144,7 @@
         if side == 0:
             own_local(matrix).wait()
             own_pair(matrix).wait_recv()
-        for sub in range(subs):
+        for sub in range(subs[stage]):
             relay(stage, sub, 0).wait_recv()
             relay(stage, sub, 1).wait_recv()
 
@@ -173,22 +175,19 @@
         lax.fori_loop(0, cols // 256, body, 0)
 
     def work(stage, sub):
-        if (stage, sub) == (0, 0):
-            place_tokens()
         if sub == 0 and stage > 0:
             ready(stage - 1)
             if stage - 1 < 6:
                 project(stage - 1)
-        quarter = heads // 8
-        if sub == subs - 1 and 3 <= stage <= 5:
-            first = (0, 3, 6)[stage - 3] * quarter // 2
-            attend(first, min(first + 3 * quarter // 2, heads // 2))
-        if stage == 6:
-            attend(heads // 2 + sub * quarter, heads // 2 + (sub + 1) * quarter)
-        if stage == 7 and sub == 0:
-            attend(heads // 2 + subs * quarter, heads)
-            combine(6)
-
+            if stage - 1 == 6:
+                attend(heads - 2, heads)
+                combine(6)
+        if sub == 0 and stage in (3, 4):
+            attend((stage - 3) * heads // 4, (stage - 2) * heads // 4)
+        if sub == 0 and stage == 6:
+            attend(heads // 2, heads - 2)
+
+    place_tokens()
     previous = None
     for message in messages:
         x_copy(*message).wait_recv()
@@ -203,7 +202,24 @@
     relay(*previous, 1).start()
     ready(7)
     combine(7)
-    u_ref[...] = rms_norm(hid_ref[...]).astype(BF16)
+    wide = hid_ref[...].astype(F32)
+    scale = lax.rsqrt(jnp.mean(wide * wide, axis=-1, keepdims=True) + EPS)
+    experts = wr_ref.shape[0]
+    logits = jnp.zeros((experts, seq), F32)
+    for start in range(0, model, 512):
+        lanes = slice(start, start + 512)
+        state = hid_ref[:, lanes].astype(F32) * scale
+        u_ref[:, lanes] = state.astype(BF16)
+        logits += lax.dot_general(wr_ref[:, lanes], state, (((1,), (1,)), ((), ())),
+                                  precision=lax.Precision.HIGHEST, preferred_element_type=F32)
+    ids = ids_ref[...]
+    numbers = lax.broadcasted_iota(jnp.int32, (experts, seq), 0)
+    chosen = numbers == ids[0:1, :]
+    for choice in range(1, ids.shape[0]):
+        chosen = jnp.logical_or(chosen, numbers == ids[choice:choice + 1, :])
+    logits = jnp.where(chosen, logits, -jnp.inf)
+    expo = jnp.exp(logits - jnp.max(logits, axis=0, keepdims=True))
+    gate_ref[...] = expo / jnp.sum(expo, axis=0, keepdims=True)
 
     oh_copy(2).wait()
     oh_copy(3).wait()
@@ -218,19 +234,20 @@
         relay(*message, 1).wait_send()
 
 
-def front(ids_lane, tokens, w_query, w_key, w_value, w_out, cap, count, head_dim):
+def front(ids_lane, tokens, router_lane, w_query, w_key, w_value, w_out, cap, count, head_dim):
     seq, model = tokens.shape
-    subs = 4
+    subs = (1, 1, 1, 1, 1, 1, 1, 2)
     vmem = pl.BlockSpec(memory_space=pltpu.VMEM)
     hbm = pl.BlockSpec(memory_space=pl.ANY)
     dma = pltpu.SemaphoreType.DMA
-    sends = 8 * subs
+    sends = sum(subs)
     return pl.pallas_call(
         functools.partial(front_kernel, subs=subs, cap=cap, count=count, head_dim=head_dim),
-        in_specs=[vmem, vmem, hbm, hbm, hbm, hbm],
-        out_specs=[vmem, vmem, vmem, hbm],
+        in_specs=[vmem, vmem, vmem, hbm, hbm, hbm, hbm],
+        out_specs=[vmem, vmem, vmem, vmem, hbm],
         out_shape=[jax.ShapeDtypeStruct((seq, model), BF16), jax.ShapeDtypeStruct((seq, model), BF16),
-                   jax.ShapeDtypeStruct((4, count, seq), jnp.int32), jax.ShapeDtypeStruct((4, seq, count * cap), BF16)],
+                   jax.ShapeDtypeStruct((4, count, seq), jnp.int32),
+                   jax.ShapeDtypeStruct((router_lane.shape[0], seq), F32), jax.ShapeDtypeStruct((4, seq, count * cap), BF16)],
         scratch_shapes=[
             pltpu.VMEM((4, model, model), BF16), pltpu.VMEM((seq, model), BF16), pltpu.VMEM((3, seq, model), BF16),
             pltpu.VMEM((seq, model), BF16), pltpu.VMEM((3,) + ids_lane.shape, jnp.int32), pltpu.VMEM((2, seq, count * cap), BF16),
@@ -238,7 +255,7 @@
             dma((2 * sends,)), dma((2 * sends,)), dma((3,)), dma((3,)), dma((2,))],
         compiler_params=pltpu.CompilerParams(collective_id=2, has_side_effects=True, vmem_limit_bytes=67043328),
         name='front',
-    )(ids_lane, tokens, w_query, w_key, w_value, w_out)
+    )(ids_lane, tokens, router_lane, w_query, w_key, w_value, w_out)
 
 
 def moe_kernel(pos_ref, u_ref, gate_ref, hid_ref, w1_ref, w3_ref, w2_ref, oh_ref, out_ref,
@@ -530,10 +547,7 @@
         cap = 2 * seq * choices // experts
         ids = expert_ids[0]
         flat = [w.reshape(w.shape[0], -1) for w in (w_query, w_key, w_value)]
-        hidden, u_own, pos, onehot = front(ids.T, tokens[0], *flat, w_out, cap, own_experts, head_dim)
-        logits = jnp.dot(rms_norm(hidden), w_router, precision=lax.Precision.HIGHEST, preferred_element_type=F32)
-        chosen = jnp.any(ids[:, :, None] == jnp.arange(experts, dtype=jnp.int32), axis=1)
-        gates = jax.nn.softmax(jnp.where(chosen, logits, -jnp.inf), axis=-1)
-        return moe(pos, u_own, gates.T, hidden, w_one, w_three, w_two, onehot, cap)[None]
+        hidden, u_own, pos, gates, onehot = front(ids.T, tokens[0], w_router.T, *flat, w_out, cap, own_experts, head_dim)
+        return moe(pos, u_own, gates, hidden, w_one, w_three, w_two, onehot, cap)[None]
 
     return jax.shard_map(local_layer, mesh=mesh, in_specs=(tok_spec, row_spec, row_spec, row_spec, row_spec, P(), row_spec, row_spec, row_spec, tok_spec), out_specs=tok_spec, check_vma=False)

time: 389 us -> 362 us (0.931)
  Pallas kernels: 361 us -> 344 us
  matrix products: 5.5 us -> 0 us
    pallas_call x1, Pallas kernels: 139 us -> 122 us  [front(): pl.pallas_call(functools.partial(front_kernel, subs=subs, cap=cap, count=...]
    dot_general x1 -> x0, matrix products: 5.5 us -> none  [local_layer(): jnp.dot(rms_norm(hidden), w_router, precision=lax.Precision.HIGHEST, pref...]
where the time goes in v5:
time: 362 us; the launch traced here: 356 us
  Pallas kernels  344 us (95%)
  local copies, waits for them, and re-layouts  10.8 us (3%)
    pallas_call x1, Pallas kernels, moe(): pl.pallas_call(functools.partial(moe_kernel, cap=cap, u_chunks=u_chunks,...  222 us
    pallas_call x1, Pallas kernels, front(): pl.pallas_call(functools.partial(front_kernel, subs=subs, cap=cap, count=...  122 us

profile of v5, /device:TPU:0, one launch (start us, length us, event | category | flops | bytes accessed | tf_op | source)
XLA Modules:
  0.0 355.5 jit_solution(15118420331214620406)
XLA Ops:
  0.0 0.0 copy-start
  0.0 0.0 copy-start.1
  0.0 3.6 %copy.17 = bf16[64,8,16,128]{3,1,2,0:T(8,128)(2,1)} copy(bf16[64,8,16,128]{3,2,1,0:T(8,128)(2,1)} %bitcast.18) | data formatting | bytes 4194304
  3.6 0.0 copy-done
  3.6 0.0 copy-done.1
  3.6 4.0 %copy_bitcast_fusion = (bf16[512,2048]{1,0:T(8,128)(2,1)}, bf16[512,2048]{1,0:T(8,128)(2,1)}) fusion(bf16[64,8,16,128]{3,2,1,0:T(8,128)(2,1)S(1)} %bitcast.19, bf16[64,8,16,128]{3,2,1,0:T(8,128)(2,1)S(1)} %bitcast.20), kind=kLoop, calls=%fused_computation | loop fusion | bytes 8388608 | tf_op jit(solution)/shard_map/reshape | solution.py:549
  7.7 122.2 %front.1 = (bf16[512,2048]{1,0:T(8,128)(2,1)}, bf16[512,2048]{1,0:T(8,128)(2,1)}, s32[4,16,512]{2,1,0:T(8,128)}, f32[64,512]{1,0:T(8,128)}, bf16[4,512,2048]{2,1,0:T(8,128)(2,1)}) custom-call(s32[8,512]{1,0:T(8,128)} %bitcast.23, bf16[512,2048]{1,0:T(8,128)(2,1)} %bitcast.21, f32[64,2048]{1,0:T(8,128)} %bitcast.22, bf16[512,2048]{1,0:T(8,128)(2,1)} %bitcast.17, ...), custom_call_target="tpu_custom_call" | custom-call | tf_op jit(solution)/shard_map/front/pallas_call | solution.py:244
  129.9 222.0 %moe.1 = bf16[512,2048]{1,0:T(8,128)(2,1)} custom-call(s32[4,16,512]{2,1,0:T(8,128)} %get-tuple-element.10.pos_ref, bf16[512,2048]{1,0:T(8,128)(2,1)} %get-tuple-element.11.u_ref, f32[64,512]{1,0:T(8,128)} %get-tuple-element.12.gate_ref, bf16[512,2048]{1,0:T(8,128)(2,1)} %get-tuple-element.13.hid_ref, bf16[16,2048,1024]{2,1,0:T(8,128)(2,1)} %w1_ref.1, ...), custom_call_target="tpu_custom_call" | custom-call | tf_op jit(solution)/shard_map/moe/pallas_call | solution.py:518
  351.9 3.2 copy.19
Async XLA Ops:
  0.0 3.6 %copy-start = (bf16[512,16,128]{2,1,0:T(8,128)(2,1)S(1)}, bf16[512,16,128]{2,1,0:T(8,128)(2,1)}, u32[]{:S(2)}) copy-start(bf16[512,16,128]{2,1,0:T(8,128)(2,1)} %param.13) | copy-start | bytes 6291460
  0.0 3.6 %copy-start.1 = (bf16[512,16,128]{2,1,0:T(8,128)(2,1)S(1)}, bf16[512,16,128]{2,1,0:T(8,128)(2,1)}, u32[]{:S(2)}) copy-start(bf16[512,16,128]{2,1,0:T(8,128)(2,1)} %param.12) | copy-start | bytes 6291460

commit v6 on v5

--- a/solution.py
+++ b/solution.py
@@ -259,7 +259,7 @@
 
 
 def moe_kernel(pos_ref, u_ref, gate_ref, hid_ref, w1_ref, w3_ref, w2_ref, oh_ref, out_ref,
-               ug, gg, rows, act, gcol, pool, oht, pst, acc, pair_buf, far_src, far_dst,
+               ug, gg, rows, raw, act, gcol, pool, oht, pst, acc, pair_buf, far_src, far_dst,
                us, ur, gs, gr, ws, ohs, ps, pr, xs, xr,
                *, cap, u_chunks, chunks, groups, wslots):
     me = lax.axis_index('ep')
@@ -326,14 +326,17 @@
         part = pl.ds(pl.multiple_of(idx * piece, piece), piece)
         return remote(ug.at[1, part], ug.at[2, part], us.at[1 + u_chunks + idx], ur.at[1 + u_chunks + idx], 0)
 
+    pair_send.start()
     for send in gate_sends:
         send.start()
     for idx in range(u_chunks):
         far_send(idx).start()
-    pair_send.start()
 
     slots = lax.broadcasted_iota(jnp.int32, (cap, seq), 0)
     lanes = lax.broadcasted_iota(jnp.int32, (cap, 128), 1)
+
+    def finish(row, slot, both):
+        act[row, :, slot * col:(slot + 1) * col] = (jax.nn.silu(both[:, :col]) * both[:, col:]).astype(BF16)
 
     def up_step(phase, index):
         first_expert = 2 * index
@@ -357,22 +360,20 @@
                 rows[0, part, :] = picked[:cap]
                 rows[1, part, :] = picked[cap:]
 
-        def finish(expert, slot, both):
-            act[phase * count + expert, :, slot * col:(slot + 1) * col] = (jax.nn.silu(both[:, :col]) * both[:, col:]).astype(BF16)
-
         for start in range(0, 2 * wslots, 2):
             for tile in (start, start + 1):
                 for copy in w13_copies(first_tile + tile):
                     copy.wait()
             if start == 0:
                 gather()
-            results = []
-            for tile in (start, start + 1):
-                idx, slot = divmod(tile, wslots)
-                results.append((first_expert + idx, slot,
-                                jnp.dot(rows[idx], pool[lax.rem(first_tile + tile, ring)], preferred_element_type=F32)))
-            for result in results:
-                finish(*result)
+            row = phase * count + first_expert
+            idx, slot = divmod(start, wslots)
+            lead = jnp.dot(rows[idx], pool[lax.rem(first_tile + start, ring)], preferred_element_type=F32)
+            last_idx, last_slot = divmod(start - 1, wslots)
+            finish(lax.rem(row + last_idx + 2 * count, 2 * count), last_slot, raw[...])
+            trail = jnp.dot(rows[idx], pool[lax.rem(first_tile + start + 1, ring)], preferred_element_type=F32)
+            finish(row + idx, slot, lead)
+            raw[...] = trail
             for tile in (start, start + 1):
                 ahead = first_tile + tile + ring
                 if phase == 0:
@@ -387,6 +388,7 @@
                         w2_start(ahead - up_tiles)
 
     gcol[...] = jnp.zeros_like(gcol)
+    raw[...] = jnp.zeros_like(raw)
     gate_sends[0].wait_recv()
     pair_send.wait_recv()
     stride = count // 2 // u_chunks
@@ -411,6 +413,7 @@
         up_step(1, index)
         return carry
     lax.fori_loop(0, count // 2, away, 0)
+    finish(2 * count - 1, wslots - 1, raw[...])
 
     total_steps = 2 * chunks * groups
 
@@ -486,7 +489,7 @@
             def _():
                 oh_copy(step + 2).start()
 
-            if part == 3:
+            if part == 2:
                 @pl.when(order > 0)
                 def _():
                     settle(order - 1)
@@ -521,7 +524,7 @@
         out_specs=vmem,
         out_shape=jax.ShapeDtypeStruct((seq, model), BF16),
         scratch_shapes=[
-            pltpu.VMEM((3, seq, model), BF16), pltpu.VMEM((3, count, seq), F32), pltpu.VMEM((2, 2 * cap, model), BF16),
+            pltpu.VMEM((3, seq, model), BF16), pltpu.VMEM((3, count, seq), F32), pltpu.VMEM((2, 2 * cap, model), BF16), pltpu.VMEM((2 * cap, block), F32),
             pltpu.VMEM((2 * count, 2 * cap, width), BF16), pltpu.VMEM((2, 2 * cap, 128), F32),
             pltpu.VMEM((6, model, block), BF16),
             pltpu.VMEM((3, 2, seq, per * cap), BF16), pltpu.VMEM((2, 2, 3 * per * cap, block), BF16),

time: 362 us -> 362 us (level)
  no operation moved by 1% of the time
where the time goes in v6:
time: 362 us; the launch traced here: 355 us
  Pallas kernels  344 us (95%)
  local copies, waits for them, and re-layouts  10.8 us (3%)
    pallas_call x1, Pallas kernels, moe(): pl.pallas_call(functools.partial(moe_kernel, cap=cap, u_chunks=u_chunks,...  222 us
    pallas_call x1, Pallas kernels, front(): pl.pallas_call(functools.partial(front_kernel, subs=subs, cap=cap, count=...  122 us

profile of v6, /device:TPU:0, one launch (start us, length us, event | category | flops | bytes accessed | tf_op | source)
XLA Modules:
  0.0 355.1 jit_solution(12878490634755538042)
XLA Ops:
  0.0 0.0 copy-start
  0.0 0.0 copy-start.1
  0.0 3.6 %copy.17 = bf16[64,8,16,128]{3,1,2,0:T(8,128)(2,1)} copy(bf16[64,8,16,128]{3,2,1,0:T(8,128)(2,1)} %bitcast.18) | data formatting | bytes 4194304
  3.6 0.0 copy-done
  3.6 0.0 copy-done.1
  3.6 4.0 %copy_bitcast_fusion = (bf16[512,2048]{1,0:T(8,128)(2,1)}, bf16[512,2048]{1,0:T(8,128)(2,1)}) fusion(bf16[64,8,16,128]{3,2,1,0:T(8,128)(2,1)S(1)} %bitcast.19, bf16[64,8,16,128]{3,2,1,0:T(8,128)(2,1)S(1)} %bitcast.20), kind=kLoop, calls=%fused_computation | loop fusion | bytes 8388608 | tf_op jit(solution)/shard_map/reshape | solution.py:552
  7.7 122.2 %front.1 = (bf16[512,2048]{1,0:T(8,128)(2,1)}, bf16[512,2048]{1,0:T(8,128)(2,1)}, s32[4,16,512]{2,1,0:T(8,128)}, f32[64,512]{1,0:T(8,128)}, bf16[4,512,2048]{2,1,0:T(8,128)(2,1)}) custom-call(s32[8,512]{1,0:T(8,128)} %bitcast.23, bf16[512,2048]{1,0:T(8,128)(2,1)} %bitcast.21, f32[64,2048]{1,0:T(8,128)} %bitcast.22, bf16[512,2048]{1,0:T(8,128)(2,1)} %bitcast.17, ...), custom_call_target="tpu_custom_call" | custom-call | tf_op jit(solution)/shard_map/front/pallas_call | solution.py:244
  129.9 221.6 %moe.1 = bf16[512,2048]{1,0:T(8,128)(2,1)} custom-call(s32[4,16,512]{2,1,0:T(8,128)} %get-tuple-element.10.pos_ref, bf16[512,2048]{1,0:T(8,128)(2,1)} %get-tuple-element.11.u_ref, f32[64,512]{1,0:T(8,128)} %get-tuple-element.12.gate_ref, bf16[512,2048]{1,0:T(8,128)(2,1)} %get-tuple-element.13.hid_ref, bf16[16,2048,1024]{2,1,0:T(8,128)(2,1)} %w1_ref.1, ...), custom_call_target="tpu_custom_call" | custom-call | tf_op jit(solution)/shard_map/moe/pallas_call | solution.py:521
  351.5 3.2 copy.19
Async XLA Ops:
  0.0 3.6 %copy-start = (bf16[512,16,128]{2,1,0:T(8,128)(2,1)S(1)}, bf16[512,16,128]{2,1,0:T(8,128)(2,1)}, u32[]{:S(2)}) copy-start(bf16[512,16,128]{2,1,0:T(8,128)(2,1)} %param.13) | copy-start | bytes 6291460
  0.0 3.6 %copy-start.1 = (bf16[512,16,128]{2,1,0:T(8,128)(2,1)S(1)}, bf16[512,16,128]{2,1,0:T(8,128)(2,1)}, u32[]{:S(2)}) copy-start(bf16[512,16,128]{2,1,0:T(8,128)(2,1)} %param.12) | copy-start | bytes 6291460
